TPU v7x, 256 devices: a whole 4x4x8 slice. The times are simulated.
256 devices in a mesh: cell: 128 (over y, x, z), gene: 2 (over core).
Axes of the slice: x: 4, y: 4, z: 8, core: 2. Of those that a mesh axis runs over, the one named last changes fastest.
Arguments:
- tiles: bfloat16 [2, 8192, 128, 128], P('gene', 'cell'), may hold values from -8 to 8
- tile_row: int32 [2, 8192], P('gene', 'cell'), may hold values from 0 to 7, as said below
- tile_col: int32 [2, 8192], P('gene', 'cell'), may hold values from 0 to 15
- tile_count: int32 [2, 128], P('gene', 'cell'), may hold values from 1 to 64, as said below
- start_basis: bfloat16 [64, 4096], P(None, 'gene'), may hold values from -0.09375 to 0.09375
Outputs:
- basis: bfloat16 [64, 131072], P(None, 'cell')
- loadings: float32 [64, 4096], P(None, ('gene', 'cell'))
Inputs may be any that keep to these rules, and one draw needn't show every extreme that they name: `tile_row`: tile row of each slot, within 0 to 7; the slots of one device name distinct (row, column) pairs. `tile_count`: slots in use; for each index of gene some device uses all 64.
All inputs are finite; a program needn't handle non-finite values.
Results may differ from a plain program's by a relative error of at most 0.018.
Values may be sent and summed in bfloat16 or wider, within the bound.
A program may use at most 64 MiB of HBM per device.

v0:
```python
import jax
import jax.numpy as jnp
from jax import lax
from jax.sharding import Mesh
from jax.sharding import PartitionSpec as P

ROW_BLOCKS = 8
CELL = ("cell_0", "cell_1", "cell_2")
GENE_CELL = ("gene", "cell_0", "cell_1", "cell_2")


def sent_to_all(value, axis):
    count = lax.axis_size(axis)
    return lax.all_to_all(
        jnp.broadcast_to(value[None], (count, *value.shape)), axis, 0, 0, tiled=True
    )


def taken_together(value, axis):
    return sent_to_all(value, axis).sum(axis=0)


def over_axes(value, axes):
    far, near = axes
    nearer = taken_together(value, near)
    return taken_together(nearer, far)


def split_up(value, dim, count):
    before, after = (value.shape[:dim], value.shape[dim + 1 :])
    return jnp.moveaxis(value.reshape(*before, count, -1, *after), dim, 0)


def sum_at_owner(value, axis, dim):
    parts = split_up(value, dim, lax.axis_size(axis))
    arrived = lax.all_to_all(parts, axis, split_axis=0, concat_axis=0, tiled=True)
    return arrived.sum(axis=0)


def sum_by_axis(value, axes, dim):
    far, near = axes
    parts = split_up(value, dim, lax.axis_size(far))
    nearer = sum_at_owner(parts, near, dim + 1)
    arrived = lax.all_to_all(nearer, far, split_axis=0, concat_axis=0, tiled=True)
    return arrived.sum(axis=0)


def padded_to(lines, count):
    spare = -len(lines) % count
    return jnp.pad(lines, [(0, spare)] + [(0, 0)] * (lines.ndim - 1))


def joined_along(parts, dim):
    lengths = list(parts.shape[1:])
    lengths[dim] *= parts.shape[0]
    return jnp.moveaxis(parts, 0, dim).reshape(lengths)


def gather_axes(value, axes, dim):
    far, near = axes
    leading = sent_to_all(value, far)
    parts = jnp.swapaxes(sent_to_all(leading, near), 0, 1)
    return joined_along(parts.reshape(-1, *value.shape), dim)


def nested_sum(value, axes):
    lines = value.reshape(-1)
    own = sum_by_axis(padded_to(lines, lax.axis_size(axes[0]) * lax.axis_size(axes[1])), axes, 0)
    whole = gather_axes(own, axes, 0)
    return whole[: len(lines)].reshape(value.shape)


def solve_lower(lower, right):
    return lax.linalg.triangular_solve(lower, right, left_side=True, lower=True)


def gram_of(scores):
    return jnp.dot(
        scores, scores.T, precision=lax.Precision.HIGHEST, preferred_element_type=jnp.float32
    )


def orthonormal(scores, first_total):
    first = first_total(gram_of(scores))
    lower_one = jnp.linalg.cholesky(first)
    return solve_lower(lower_one, scores)


def local(tiles, tile_row, tile_col, tile_count, start_basis):
    blocks_local = tiles[0]
    slot_count = blocks_local.shape[0]
    tile_size = blocks_local.shape[-1]
    width = start_basis.shape[0]
    gene_dev = start_basis.shape[1]
    gene_blocks = gene_dev // tile_size
    row_blocks = ROW_BLOCKS
    cell_dev = row_blocks * tile_size
    row_index = tile_row[0]
    col_index = tile_col[0]
    live = jnp.arange(slot_count) < tile_count[0, 0]
    row_target = jnp.where(live, row_index, row_blocks)
    col_target = jnp.where(live, col_index, gene_blocks)

    def first_total(gram):
        return over_axes(gram, ("cell_0", ("cell_1", "cell_2")))

    def merge_halves(partial_scores):
        return taken_together(partial_scores, "gene")

    def scores_of(basis):
        picked = jnp.take(basis.reshape(width, gene_blocks, tile_size), col_index, axis=1)
        products = jnp.einsum(
            "ksg,srg->skr", picked, blocks_local, preferred_element_type=jnp.float32
        )
        summed = jax.ops.segment_sum(products, row_target, num_segments=row_blocks + 1)[:row_blocks]
        return merge_halves(jnp.transpose(summed, (1, 0, 2)).reshape(width, cell_dev))

    def loadings_of(ortho_half):
        picked = jnp.take(ortho_half.reshape(width, row_blocks, tile_size), row_index, axis=1)
        products = jnp.einsum(
            "ksr,srg->skg", picked, blocks_local, preferred_element_type=jnp.float32
        )
        summed = jax.ops.segment_sum(products, col_target, num_segments=gene_blocks + 1)[
            :gene_blocks
        ]
        return jnp.transpose(summed, (1, 0, 2)).reshape(width, gene_dev)

    ortho = orthonormal(scores_of(start_basis), first_total)
    ortho_half = ortho.astype(jnp.bfloat16)
    partial_value = loadings_of(ortho_half)
    next_basis = nested_sum(partial_value, ("cell_0", ("cell_1", "cell_2"))).astype(jnp.bfloat16)
    ortho_two = orthonormal(scores_of(next_basis), first_total)
    scale = jnp.sqrt(jnp.float32(lax.axis_size(CELL) * cell_dev))
    ortho_two_half = ortho_two.astype(jnp.bfloat16)
    basis_piece = (ortho_two * scale).astype(jnp.bfloat16)
    basis = basis_piece
    loadings = sum_by_axis(loadings_of(ortho_two_half), ("cell_0", ("cell_1", "cell_2")), 1)
    return (basis, loadings)


def solution(mesh):
    finer = Mesh(
        mesh.devices.reshape(4, 4, 8, mesh.shape["gene"]), ("cell_0", "cell_1", "cell_2", "gene")
    )
    return jax.shard_map(
        local,
        mesh=finer,
        in_specs=(
            P("gene", CELL, None, None),
            P("gene", CELL),
            P("gene", CELL),
            P("gene", CELL),
            P(None, "gene"),
        ),
        out_specs=(P(None, CELL), P(None, GENE_CELL)),
        check_vma=False,
    )
```

profile of v0, /device:TPU:32, one launch (start us, length us, event | category | flops | bytes accessed | tf_op | source)
XLA Modules:
  0.0 259.6 jit_solution(13456139225536636353)
XLA Ops:
  0.7 0.8 compare_select_fusion
  1.5 0.7 compare_and_fusion
  2.1 1.0 copy_bitcast_fusion.2
  3.8 0.7 gather_fusion
  4.6 2.9 %fusion.6 = f32[64,64,128]{2,1,0:T(8,128)} fusion(bf16[1,64,128,128]{3,2,1,0:T(8,128)(2,1)S(1)} %copy-done, bf16[64,64,128]{2,1,0:T(8,128)(2,1)S(1)} %gather_fusion, pred[64]{0:T(512)(128)(4,1)S(1)} %compare_and_fusion), kind=kOutput, calls=%fused_computation.14 | convolution fusion | flops 134742016 | bytes 5242944 | tf_op jit(solution)/shard_map/ksg,srg->skr/dot_general | solution.py:112
  7.5 7.1 %scatter_fusion = f32[9,64,128]{2,1,0:T(8,128)S(1)} fusion(f32[9,64,128]{2,1,0:T(8,128)S(1)} %broadcast.76.clone, s32[64]{0:T(128)S(1)} %get-tuple-element.8, f32[64,64,128]{2,1,0:T(8,128)} %fusion.6), kind=kCustom, calls=%fused_computation.4 | custom fusion | flops 524288 | bytes 6291712 | tf_op jit(solution)/shard_map/scatter-add | solution.py:115
  14.7 4.2 %all_to_all.69 = f32[2,64,1024]{2,1,0:T(8,128)S(1)} all-to-all(f32[2,64,1024]{2,1,0:T(8,128)S(1)} %broadcast_in_dim.85), channel_id=1, replica_groups=mesh['cell_0'=4,'cell_1'=4,'cell_2'=8,'gene'=2] {'gene'}, dimensions={0} | all-to-all | bytes 1048576 | tf_op jit(solution)/shard_map/all_to_all | solution.py:14
  18.9 0.4 fusion.42
  19.4 1.4 reshape.171
  20.8 11.2 %all-to-all-start.1 = ((f32[32,1,4096]{2,1,0:T(1,128)}), f32[32,1,4096]{2,1,0:T(1,128)S(1)}, u32[]{:S(2)}, u32[]{:S(2)}) async-start(f32[32,1,4096]{2,1,0:T(1,128)} %reshape.171), calls=%async_computation.1 | async-start | bytes 1048576 | tf_op jit(solution)/shard_map/all_to_all | solution.py:14
  32.0 17.9 %all-to-all-done.1 = f32[32,1,4096]{2,1,0:T(1,128)S(1)} async-done(((f32[32,1,4096]{2,1,0:T(1,128)}), f32[32,1,4096]{2,1,0:T(1,128)S(1)}, u32[]{:S(2)}, u32[]{:S(2)}) %all-to-all-start.1) | async-done | bytes 524320 | tf_op jit(solution)/shard_map/all_to_all | solution.py:14
  49.9 0.5 broadcast.145
  50.4 2.8 %reduce.5 = f32[32,4096]{1,0:T(8,128)} reduce(f32[32,1,4096]{2,1,0:T(1,128)S(1)} %all-to-all-done.1, f32[]{:T(128)} %broadcast.145), dimensions={1}, to_apply=%all_to_all.41.reduce_sub_computation | reduce | bytes 1048580 | tf_op jit(solution)/shard_map/all_to_all | solution.py:14
  53.2 1.5 reshape.172
  54.8 0.8 reshape.173
  55.5 4.5 %all-to-all-start.2 = ((f32[4,1,4096]{2,1,0:T(1,128)}), f32[4,1,4096]{2,1,0:T(1,128)S(1)}, u32[]{:S(2)}, u32[]{:S(2)}) async-start(f32[4,1,4096]{2,1,0:T(1,128)} %reshape.173), calls=%async_computation.2 | async-start | bytes 131072 | tf_op jit(solution)/shard_map/all_to_all | solution.py:14
  60.0 5.6 %all-to-all-done.2 = f32[4,1,4096]{2,1,0:T(1,128)S(1)} async-done(((f32[4,1,4096]{2,1,0:T(1,128)}), f32[4,1,4096]{2,1,0:T(1,128)S(1)}, u32[]{:S(2)}, u32[]{:S(2)}) %all-to-all-start.2) | async-done | bytes 65568 | tf_op jit(solution)/shard_map/all_to_all | solution.py:14
  65.6 0.8 reduce.6
  66.7 5.8 %cholesky.44 = f32[64,64]{1,0:T(8,128)S(1)} custom-call(f32[64,64]{1,0:T(8,128)S(1)} %fusion.31), custom_call_target="Cholesky" | custom-call | tf_op jit(solution)/shard_map/jit(cholesky)/cholesky | solution.py:85
  72.6 0.6 compare_reduce_fusion.1
  73.2 0.7 fusion.25
  73.9 4.9 %custom-call.6 = f32[1,64,64]{1,2,0:T(8,128)S(1)} custom-call(f32[1,64,64]{2,1,0:T(8,128)S(1)} %fusion.25), custom_call_target="InvertDiagBlocksLowerTriangular" | custom-call | tf_op jit(solution)/shard_map/triangular_solve/custom-call.0 | solution.py:74
  78.8 0.4 fusion.8
  79.2 0.7 gather_fusion.1
  80.0 2.1 fusion.4
  82.1 7.1 %scatter_fusion.1 = f32[17,64,128]{2,1,0:T(8,128)S(1)} fusion(f32[17,64,128]{2,1,0:T(8,128)S(1)} %broadcast.77.clone, s32[64]{0:T(128)S(1)} %get-tuple-element.9, f32[64,64,128]{2,1,0:T(8,128)} %fusion.4), kind=kCustom, calls=%fused_computation.5 | custom fusion | flops 524288 | bytes 6291712 | tf_op jit(solution)/shard_map/scatter-add | solution.py:123
  89.2 0.3 copy.45
  89.6 0.3 copy.46
  90.0 20.6 %all_to_all.70 = f32[32,4,1024]{2,1,0:T(4,128)S(1)} all-to-all(f32[32,4,1024]{2,1,0:T(4,128)S(1)} %copy.46), channel_id=1, replica_groups=mesh['cell_0'=4,'cell_1'=4,'cell_2'=8,'gene'=2] {'cell_1','cell_2'}, dimensions={0} | all-to-all | bytes 1048576 | tf_op jit(solution)/shard_map/all_to_all | solution.py:36
  110.7 7.7 %all_to_all.71 = f32[4,1,1024]{2,1,0:T(1,128)S(1)} all-to-all(f32[4,1,1024]{2,1,0:T(1,128)S(1)} %all_to_all.44), channel_id=1, replica_groups=mesh['cell_0'=4,'cell_1'=4,'cell_2'=8,'gene'=2] {'cell_0'}, dimensions={0} | all-to-all | bytes 32768 | tf_op jit(solution)/shard_map/all_to_all | solution.py:44
  118.5 0.5 broadcast.147
  119.0 0.7 reduce.7
  119.7 7.7 %all_to_all.65 = bf16[4,2,512]{2,1,0:T(2,128)(2,1)S(1)} all-to-all(bf16[4,2,512]{2,1,0:T(2,128)(2,1)S(1)} %reshape.175), channel_id=1, replica_groups=mesh['cell_0'=4,'cell_1'=4,'cell_2'=8,'gene'=2] {'cell_0'}, dimensions={0} | all-to-all | bytes 16384 | tf_op jit(solution)/shard_map/all_to_all | solution.py:14
  127.5 15.6 %all_to_all.72 = bf16[32,4,1024]{2,1,0:T(4,128)(2,1)S(1)} all-to-all(bf16[32,4,1024]{2,1,0:T(4,128)(2,1)S(1)} %broadcast_in_dim.90), channel_id=1, replica_groups=mesh['cell_0'=4,'cell_1'=4,'cell_2'=8,'gene'=2] {'cell_1','cell_2'}, dimensions={0} | all-to-all | bytes 524288 | tf_op jit(solution)/shard_map/all_to_all | solution.py:14
  143.4 0.7 gather_fusion.2
  144.2 2.9 %fusion.2 = f32[64,64,128]{2,1,0:T(8,128)} fusion(bf16[1,64,128,128]{3,2,1,0:T(8,128)(2,1)S(1)} %copy-done, bf16[64,64,128]{2,1,0:T(8,128)(2,1)S(1)} %gather_fusion.2, pred[64]{0:T(512)(128)(4,1)S(1)} %compare_and_fusion), kind=kOutput, calls=%fused_computation.10 | convolution fusion | flops 134742016 | bytes 5242944 | tf_op jit(solution)/shard_map/ksg,srg->skr/dot_general | solution.py:112
  147.1 7.1 %scatter_fusion.2 = f32[9,64,128]{2,1,0:T(8,128)S(1)} fusion(f32[9,64,128]{2,1,0:T(8,128)S(1)} %broadcast.76, s32[64]{0:T(128)S(1)} %get-tuple-element.8, f32[64,64,128]{2,1,0:T(8,128)} %fusion.2), kind=kCustom, calls=%fused_computation.6 | custom fusion | flops 524288 | bytes 6291712 | tf_op jit(solution)/shard_map/scatter-add | solution.py:115
  154.3 4.2 %all_to_all.66 = f32[2,64,1024]{2,1,0:T(8,128)S(1)} all-to-all(f32[2,64,1024]{2,1,0:T(8,128)S(1)} %broadcast_in_dim.92), channel_id=1, replica_groups=mesh['cell_0'=4,'cell_1'=4,'cell_2'=8,'gene'=2] {'gene'}, dimensions={0} | all-to-all | bytes 1048576 | tf_op jit(solution)/shard_map/all_to_all | solution.py:14
  158.4 0.4 fusion.43
  158.9 1.4 reshape.177
  160.4 22.4 %all_to_all.73 = f32[32,1,4096]{2,1,0:T(1,128)S(1)} all-to-all(f32[32,1,4096]{2,1,0:T(1,128)} %reshape.177), channel_id=1, replica_groups=mesh['cell_0'=4,'cell_1'=4,'cell_2'=8,'gene'=2] {'cell_1','cell_2'}, dimensions={0} | all-to-all | bytes 1048576 | tf_op jit(solution)/shard_map/all_to_all | solution.py:14
  182.8 2.8 %reduce.8 = f32[32,4096]{1,0:T(8,128)} reduce(f32[32,1,4096]{2,1,0:T(1,128)S(1)} %all_to_all.73, f32[]{:T(128)} %broadcast.145), dimensions={1}, to_apply=%all_to_all.49.reduce_sub_computation | reduce | bytes 1048580 | tf_op jit(solution)/shard_map/all_to_all | solution.py:14
  185.5 1.5 reshape.178
  187.2 8.0 %all_to_all.74 = f32[4,1,4096]{2,1,0:T(1,128)S(1)} all-to-all(f32[4,1,4096]{2,1,0:T(1,128)S(1)} %reshape.179), channel_id=1, replica_groups=mesh['cell_0'=4,'cell_1'=4,'cell_2'=8,'gene'=2] {'cell_0'}, dimensions={0} | all-to-all | bytes 131072 | tf_op jit(solution)/shard_map/all_to_all | solution.py:14
  195.2 0.8 reduce.9
  196.3 5.8 %cholesky.55 = f32[64,64]{1,0:T(8,128)S(1)} custom-call(f32[64,64]{1,0:T(8,128)S(1)} %fusion.29), custom_call_target="Cholesky" | custom-call | tf_op jit(solution)/shard_map/jit(cholesky)/cholesky | solution.py:85
  202.2 0.6 compare_reduce_fusion
  202.8 0.7 fusion.26
  203.5 4.9 %custom-call.7 = f32[1,64,64]{1,2,0:T(8,128)S(1)} custom-call(f32[1,64,64]{2,1,0:T(8,128)S(1)} %fusion.26), custom_call_target="InvertDiagBlocksLowerTriangular" | custom-call | tf_op jit(solution)/shard_map/triangular_solve/custom-call.0 | solution.py:74
  208.4 1.1 convert_bitcast_fusion.1
  209.5 0.7 gather_fusion.3
  210.2 2.1 fusion
  212.4 7.1 %scatter_fusion.3 = f32[17,64,128]{2,1,0:T(8,128)S(1)} fusion(f32[17,64,128]{2,1,0:T(8,128)S(1)} %broadcast.77, s32[64]{0:T(128)S(1)} %get-tuple-element.9, f32[64,64,128]{2,1,0:T(8,128)} %fusion), kind=kCustom, calls=%fused_computation.7 | custom fusion | flops 524288 | bytes 6291712 | tf_op jit(solution)/shard_map/scatter-add | solution.py:123
  219.5 0.3 copy.52
  219.8 1.0 reshape_reshape.8
  220.8 1.4 copy.53
  222.2 1.1 copy.73
  223.3 1.9 reshape.181
  225.2 20.9 %all_to_all.67 = f32[32,1,4096]{2,1,0:T(1,128)S(1)} all-to-all(f32[32,1,4096]{2,1,0:T(1,128)S(1)} %reshape.181), channel_id=1, replica_groups=mesh['cell_0'=4,'cell_1'=4,'cell_2'=8,'gene'=2] {'cell_1','cell_2'}, dimensions={0} | all-to-all | bytes 1048576 | tf_op jit(solution)/shard_map/all_to_all | solution.py:36
  246.1 2.8 %reduce.10 = f32[32,4096]{1,0:T(8,128)} reduce(f32[32,1,4096]{2,1,0:T(1,128)S(1)} %all_to_all.67, f32[]{:T(128)} %broadcast.145), dimensions={1}, to_apply=%all_to_all.51.reduce_sub_computation | reduce | bytes 1048580 | tf_op jit(solution)/shard_map/all_to_all | solution.py:36
  248.8 1.5 reshape.182
  250.5 7.7 %all_to_all.68 = f32[4,1,1024]{2,1,0:T(1,128)S(1)} all-to-all(f32[4,1,1024]{2,1,0:T(1,128)S(1)} %reshape.183), channel_id=1, replica_groups=mesh['cell_0'=4,'cell_1'=4,'cell_2'=8,'gene'=2] {'cell_0'}, dimensions={0} | all-to-all | bytes 32768 | tf_op jit(solution)/shard_map/all_to_all | solution.py:44
  258.2 0.7 reduce.11
  259.0 0.6 bitcast_reduce_fusion.1
  (57 shorter events, 2.4 us)
Async XLA Ops:
  0.6 4.0 %copy-start = (bf16[1,64,128,128]{3,2,1,0:T(8,128)(2,1)S(1)}, bf16[1,64,128,128]{3,2,1,0:T(8,128)(2,1)}, u32[]{:S(2)}) copy-start(bf16[1,64,128,128]{3,2,1,0:T(8,128)(2,1)} %param.12) | copy-start | bytes 6291460
  0.6 3.9 %copy-start.1 = (s32[1,64]{1,0:T(1,128)S(1)}, s32[1,64]{1,0:T(1,128)}, u32[]{:S(2)}) copy-start(s32[1,64]{1,0:T(1,128)} %param.14) | copy-start | bytes 772
  0.7 3.9 %copy-start.2 = (s32[1,64]{1,0:T(1,128)S(1)}, s32[1,64]{1,0:T(1,128)}, u32[]{:S(2)}) copy-start(s32[1,64]{1,0:T(1,128)} %param.13) | copy-start | bytes 772
  20.8 29.1 %all-to-all-start.1 = ((f32[32,1,4096]{2,1,0:T(1,128)}), f32[32,1,4096]{2,1,0:T(1,128)S(1)}, u32[]{:S(2)}, u32[]{:S(2)}) async-start(f32[32,1,4096]{2,1,0:T(1,128)} %reshape.171), calls=%async_computation.1 | async-start | bytes 1048576 | tf_op jit(solution)/shard_map/all_to_all | solution.py:14
  55.5 10.1 %all-to-all-start.2 = ((f32[4,1,4096]{2,1,0:T(1,128)}), f32[4,1,4096]{2,1,0:T(1,128)S(1)}, u32[]{:S(2)}, u32[]{:S(2)}) async-start(f32[4,1,4096]{2,1,0:T(1,128)} %reshape.173), calls=%async_computation.2 | async-start | bytes 131072 | tf_op jit(solution)/shard_map/all_to_all | solution.py:14
where the time goes:
time: 261 us; the launch traced here: 260 us
  blocking collectives  119 us (46%)
  other arithmetic  66.3 us (25%)
  waiting for transfers between devices  23.5 us (9%)
  local copies, waits for them, and re-layouts  21.2 us (8%)
  starting transfers between devices  15.6 us (6%)
  matrix products  12.2 us (5%)
    all_to_all x6, blocking collectives, sent_to_all(): lax.all_to_all(jnp.broadcast_to(value[None], (count, *value.shape)), axis...  62 us
    all_to_all x2, blocking collectives, sum_at_owner(): lax.all_to_all(parts, axis, split_axis=0, concat_axis=0, tiled=True)  41.5 us
    all_to_all x2, waiting for transfers between devices, sent_to_all(): lax.all_to_all(jnp.broadcast_to(value[None], (count, *value.shape)), axis...  23.5 us
    all_to_all x2, starting transfers between devices, sent_to_all(): lax.all_to_all(jnp.broadcast_to(value[None], (count, *value.shape)), axis...  15.6 us
    all_to_all x2, blocking collectives, sum_by_axis(): lax.all_to_all(nearer, far, split_axis=0, concat_axis=0, tiled=True)  15.4 us
    scatter-add x2, other arithmetic, scores_of(): jax.ops.segment_sum(products, row_target, num_segments=row_blocks + 1)  14.1 us
    scatter-add x2, other arithmetic, loadings_of(): jax.ops.segment_sum(products, col_target, num_segments=gene_blocks + 1)  14.1 us
    another operation x6, other arithmetic, orthonormal(): lower_one = jnp.linalg.cholesky(first)  13 us
  transfers between devices with their start and end apart: 2, of which 2 were waited for; matrix products, arithmetic and copies ran while one was open for 0% of the time, Pallas kernels for 0%

commit v1 on v0

v1 whole, which is shorter than its diff:
```python
import jax
import jax.numpy as jnp
from jax import lax
from jax.experimental import pallas as pl
from jax.experimental.pallas import tpu as pltpu
from jax.sharding import Mesh
from jax.sharding import PartitionSpec as P

K = 64
TILE = 128
ROW_BLOCKS = 8
COL_BLOCKS = 16
SLOTS = 64
CELLS = ROW_BLOCKS * TILE
GENES = COL_BLOCKS * TILE
NY, NX, NZ = 4, 4, 8
TOTAL_CELLS = NY * NX * NZ * CELLS
CELL = ("cell_0", "cell_1", "cell_2")
GENE_CELL = ("gene", "cell_0", "cell_1", "cell_2")
MESH = pl.DeviceIdType.MESH
F32 = jnp.float32
BF16 = jnp.bfloat16
HIGHEST = lax.Precision.HIGHEST
LANES = (((1,), (1,)), ((), ()))

PAIR, FIRST, SECOND, DEEP, GDEEP, GFIRST, GSECOND = 0, 1, 4, 7, 14, 21, 24
PER_ROUND = 27
ZGATHER, BGATHER, AGATHER = 54, 61, 64
MESSAGES = 67


def invert(gram):
    eye = (
        lax.broadcasted_iota(jnp.int32, (K, K), 0) == lax.broadcasted_iota(jnp.int32, (K, K), 1)
    ).astype(F32)
    both = jnp.concatenate([gram, eye], axis=1)
    parts = [both[8 * i : 8 * i + 8] for i in range(K // 8)]
    inner = lax.broadcasted_iota(jnp.int32, (8, 1), 0)
    scales = []
    for j in range(K):
        at, row = divmod(j, 8)
        pivot_row = parts[at][row : row + 1, :]
        pivot = pivot_row[:, j : j + 1]
        over = pivot_row * (1.0 / pivot)
        scales.append(lax.rsqrt(pivot))
        for i in range(at, K // 8):
            column = parts[i][:, j : j + 1]
            if i == at:
                column = jnp.where(inner > row, column, 0.0)
            parts[i] = parts[i] - column * over
    out = []
    for i in range(K // 8):
        scale = jnp.zeros((8, 1), F32)
        for r in range(8):
            scale = jnp.where(inner == r, scales[8 * i + r], scale)
        out.append(parts[i][:, K:] * scale)
    return jnp.concatenate(out, axis=0)


def kernel(
    inverse, tiles_any, start_ref, basis_ref, loadings_ref,
    tiles, x_ref, own, other, product, first, plane, second, deep, deep_in,
    gram, gdeep, gfirst, gsecond, gathered, mid, tile_sem, send_sem, recv_sem,
):
    y, x, z = (lax.axis_index(name) for name in CELL)
    core = lax.axis_index("gene")
    swap = 1 - core
    a = y * swap + x * core
    b = x * swap + y * core

    def on_a(d):
        at = lax.rem(a + d, 4)
        return at, (at * swap + y * core, x * swap + at * core, z, core)

    def on_b(d):
        at = lax.rem(b + d, 4)
        return at, (y * swap + at * core, at * swap + x * core, z, core)

    def on_z(d):
        at = lax.rem(z + d, NZ)
        return at, (y, x, at, core)

    partner = (y, x, z, swap)
    load = pltpu.make_async_copy(tiles_any, tiles.at[pl.ds(0, SLOTS)], tile_sem)
    load.start()

    barrier = pltpu.get_barrier_semaphore()
    peers = [partner]
    peers += [on_a(d)[1] for d in range(1, 4)] + [on_b(d)[1] for d in range(1, 4)]
    peers += [on_z(d)[1] for d in range(1, NZ)]
    for peer in peers:
        pl.semaphore_signal(barrier, inc=1, device_id=peer, device_id_type=MESH)

    tiles[SLOTS] = jnp.zeros((TILE, TILE), BF16)
    load.wait()

    def build(r, carry):
        for c in range(COL_BLOCKS):
            x_ref[pl.ds(pl.multiple_of(r * TILE, TILE), TILE), pl.ds(c * TILE, TILE)] = tiles[
                inverse[r * COL_BLOCKS + c]
            ]
        return carry

    lax.fori_loop(0, ROW_BLOCKS, build, 0)

    sent = []

    def send(src, dst, number, peer):
        copy = pltpu.make_async_remote_copy(
            src_ref=src, dst_ref=dst, send_sem=send_sem.at[number], recv_sem=recv_sem.at[number],
            device_id=peer, device_id_type=MESH,
        )
        copy.start()
        sent.append(copy)
        return copy

    def arrive(copies):
        for copy in copies:
            copy.wait_recv()

    def stored(yy, xx):
        return swap * (4 * yy + xx) + core * (4 * xx + yy)

    def round_of(r, basis):
        base = r * PER_ROUND
        own[r] = lax.dot_general(basis, x_ref[...], LANES, preferred_element_type=F32)
        if r == 0:
            pl.semaphore_wait(barrier, len(peers))
        arrive([send(own.at[r], other.at[r], base + PAIR, partner)])
        scores = own[r] + other[r]
        square = lax.dot_general(
            scores, jnp.concatenate([scores, scores], axis=0), LANES,
            precision=HIGHEST, preferred_element_type=F32,
        )
        half = lax.broadcasted_iota(jnp.int32, (K // 2, 2 * K), 1) < K
        gram[r, 0] = jnp.where(half, square[: K // 2], square[K // 2 :])
        gdeep_in = [
            send(gram.at[r, 0], gdeep.at[r, d - 1], base + GDEEP + d - 1, on_z(d)[1]) for d in range(1, NZ)
        ]
        high = scores.astype(BF16)
        low = (scores - high.astype(F32)).astype(BF16)
        doubled = jnp.dot(
            jnp.concatenate([high, low], axis=0), x_ref[...], preferred_element_type=F32
        )
        summed = doubled[:K] + doubled[K:]
        for yy in range(NY):
            for xx in range(NX):
                n = NX * yy + xx
                product[r, stored(yy, xx)] = summed[:, n * TILE : (n + 1) * TILE]
        came = []
        for d in range(1, 4):
            at, peer = on_a(d)
            came.append(send(product.at[r, pl.ds(4 * at, 4)], first.at[r, d - 1], base + FIRST + d - 1, peer))
        arrive(came)
        for j in range(4):
            plane[r, j] = product[r, 4 * a + j] + first[r, 0, j] + first[r, 1, j] + first[r, 2, j]
        came = []
        for d in range(1, 4):
            at, peer = on_b(d)
            came.append(send(plane.at[r, at], second.at[r, d - 1], base + SECOND + d - 1, peer))
        arrive(gdeep_in)
        total = gram[r, 0]
        for d in range(NZ - 1):
            total = total + gdeep[r, d]
        gram[r, 1] = total
        gcame = [send(gram.at[r, 1], gfirst.at[r, d - 1], base + GFIRST + d - 1, on_a(d)[1]) for d in range(1, 4)]
        arrive(came)
        column = plane[r, b] + second[r, 0] + second[r, 1] + second[r, 2]
        turned = jnp.transpose(jnp.concatenate([column, column], axis=0))
        lane_half = lax.broadcasted_iota(jnp.int32, (8, 2 * K), 1) < K
        for zz in range(NZ):
            deep[r, zz] = jnp.where(lane_half, turned[16 * zz : 16 * zz + 8], turned[16 * zz + 8 : 16 * zz + 16])
        came = []
        for d in range(1, NZ):
            at, peer = on_z(d)
            came.append(send(deep.at[r, at], deep_in.at[r, d - 1], base + DEEP + d - 1, peer))
        arrive(gcame)
        gram[r, 2] = gram[r, 1] + gfirst[r, 0] + gfirst[r, 1] + gfirst[r, 2]
        gcame = [send(gram.at[r, 2], gsecond.at[r, d - 1], base + GSECOND + d - 1, on_b(d)[1]) for d in range(1, 4)]
        arrive(gcame)
        packed = gram[r, 2] + gsecond[r, 0] + gsecond[r, 1] + gsecond[r, 2]
        whole = jnp.concatenate([packed[:, :K], packed[:, K:]], axis=0)
        arrive(came)
        piece = deep[r, z]
        for d in range(NZ - 1):
            piece = piece + deep_in[r, d]
        return scores, whole, piece

    def unpacked(piece):
        return jnp.concatenate([piece[:, :K], piece[:, K:]], axis=0)

    _, whole, piece = round_of(0, start_ref[...])
    gathered[z] = piece
    came = [send(gathered.at[z], gathered.at[z], ZGATHER + d - 1, on_z(d)[1]) for d in range(1, NZ)]
    lower = invert(whole)
    arrive(came)
    genes = jnp.concatenate([unpacked(gathered[zz]) for zz in range(NZ)], axis=0)
    middle = lax.dot_general(lower, genes, LANES, precision=HIGHEST, preferred_element_type=F32)
    mine = 4 * a + b
    mid[mine] = middle.astype(BF16)
    came = [send(mid.at[mine], mid.at[mine], BGATHER + d - 1, on_b(d)[1]) for d in range(1, 4)]
    arrive(came)
    rows = pl.ds(4 * a, 4)
    came = [send(mid.at[rows], mid.at[rows], AGATHER + d - 1, on_a(d)[1]) for d in range(1, 4)]
    arrive(came)
    basis = jnp.concatenate([mid[stored(n // NX, n % NX)] for n in range(NY * NX)], axis=1)

    scores, whole, piece = round_of(1, basis)
    lower = invert(whole)
    ortho = jnp.dot(lower, scores, precision=HIGHEST, preferred_element_type=F32)
    basis_ref[...] = (ortho * jnp.sqrt(F32(TOTAL_CELLS))).astype(BF16)
    loadings_ref[...] = lax.dot_general(
        lower, unpacked(piece), LANES, precision=HIGHEST, preferred_element_type=F32
    )
    for copy in sent:
        copy.wait_send()


def local(tiles, tile_row, tile_col, tile_count, start_basis):
    places = ROW_BLOCKS * COL_BLOCKS
    slot = jnp.arange(SLOTS, dtype=jnp.int32)
    place = jnp.where(slot < tile_count[0, 0], tile_row[0] * COL_BLOCKS + tile_col[0], places)
    hit = place[None, :] == jnp.arange(places, dtype=jnp.int32)[:, None]
    inverse = jnp.min(jnp.where(hit, slot[None, :], SLOTS), axis=1)
    vmem = pl.BlockSpec(memory_space=pltpu.VMEM)
    basis, loadings = pl.pallas_call(
        kernel,
        out_shape=(
            jax.ShapeDtypeStruct((K, CELLS), BF16),
            jax.ShapeDtypeStruct((K, GENES // (NY * NX * NZ)), F32),
        ),
        in_specs=[pl.BlockSpec(memory_space=pltpu.SMEM), pl.BlockSpec(memory_space=pl.ANY), vmem],
        out_specs=(vmem, vmem),
        scratch_shapes=[
            pltpu.VMEM((SLOTS + 1, TILE, TILE), BF16),
            pltpu.VMEM((CELLS, GENES), BF16),
            pltpu.VMEM((2, K, CELLS), F32),
            pltpu.VMEM((2, K, CELLS), F32),
            pltpu.VMEM((2, NY * NX, K, TILE), F32),
            pltpu.VMEM((2, 3, 4, K, TILE), F32),
            pltpu.VMEM((2, 4, K, TILE), F32),
            pltpu.VMEM((2, 3, K, TILE), F32),
            pltpu.VMEM((2, NZ, 8, TILE), F32),
            pltpu.VMEM((2, NZ - 1, 8, TILE), F32),
            pltpu.VMEM((2, 3, K // 2, 2 * K), F32),
            pltpu.VMEM((2, NZ - 1, K // 2, 2 * K), F32),
            pltpu.VMEM((2, 3, K // 2, 2 * K), F32),
            pltpu.VMEM((2, 3, K // 2, 2 * K), F32),
            pltpu.VMEM((NZ, 8, TILE), F32),
            pltpu.VMEM((NY * NX, K, TILE), BF16),
            pltpu.SemaphoreType.DMA,
            pltpu.SemaphoreType.DMA((MESSAGES,)),
            pltpu.SemaphoreType.DMA((MESSAGES,)),
        ],
        compiler_params=pltpu.CompilerParams(collective_id=0, has_side_effects=True),
    )(inverse, tiles[0], start_basis)
    return basis, loadings


def solution(mesh):
    finer = Mesh(
        mesh.devices.reshape(NY, NX, NZ, mesh.shape["gene"]), ("cell_0", "cell_1", "cell_2", "gene")
    )
    return jax.shard_map(
        local,
        mesh=finer,
        in_specs=(
            P("gene", CELL, None, None),
            P("gene", CELL),
            P("gene", CELL),
            P("gene", CELL),
            P(None, "gene"),
        ),
        out_specs=(P(None, CELL), P(None, GENE_CELL)),
        check_vma=False,
    )
```

time: 261 us -> 81.1 us (0.31)
  the two profiles are of different devices: /device:TPU:32 before, /device:TPU:1 now
where the time goes in v1:
time: 81.1 us; the launch traced here: 80.9 us
  Pallas kernels  75.3 us (93%)
  local copies, waits for them, and re-layouts  2.99 us (4%)
  between operations  1.29 us (2%)
  other arithmetic  1.28 us (2%)
    pallas_call x1, Pallas kernels, local(): pl.pallas_call(kernel, out_shape=(jax.ShapeDtypeStruct((K, CELLS), BF16),...  75.3 us

profile of v1, /device:TPU:1, one launch (start us, length us, event | category | flops | bytes accessed | tf_op | source)
XLA Modules:
  0.0 80.9 jit_solution(882981246776272864)
XLA Ops:
  1.3 0.7 fusion
  2.0 0.6 select_reduce_fusion.inverse
  2.6 75.3 %shard_map.68 = (bf16[64,1024]{1,0:T(8,128)(2,1)}, f32[64,16]{1,0:T(8,128)}) custom-call(s32[128]{0:T(128)} %select_reduce_fusion.inverse, bf16[64,128,128]{2,1,0:T(8,128)(2,1)} %bitcast.5, bf16[64,2048]{1,0:T(8,128)(2,1)} %start_ref.1), custom_call_target="tpu_custom_call" | custom-call | tf_op jit(solution)/shard_map/pallas_call | solution.py:226
  77.9 1.4 %copy.8 = f32[64,16]{0,1:T(8,128)} copy(f32[64,16]{1,0:T(8,128)} %get-tuple-element.5) | data formatting | bytes 8192 | tf_op jit(solution)/shard_map/pallas_call | solution.py:226
  79.3 1.6 %copy.11 = bf16[64,1024]{1,0:T(8,128)(2,1)} copy(bf16[64,1024]{1,0:T(8,128)(2,1)} %get-tuple-element.8) | data formatting | bytes 262144

commit v2 on v0

v2 whole, which is shorter than its diff:
```python
import jax
import jax.numpy as jnp
from jax import lax
from jax.experimental import pallas as pl
from jax.experimental.pallas import tpu as pltpu
from jax.sharding import Mesh
from jax.sharding import PartitionSpec as P

K = 64
TILE = 128
ROW_BLOCKS = 8
COL_BLOCKS = 16
SLOTS = 64
CELLS = ROW_BLOCKS * TILE
GENES = COL_BLOCKS * TILE
NY, NX, NZ = 4, 4, 8
PLANE = NY * NX
CHUNKS = 4
CHUNK = CELLS // CHUNKS
PAIRS = COL_BLOCKS // 2
TOTAL_CELLS = PLANE * NZ * CELLS
CELL = ("cell_0", "cell_1", "cell_2")
GENE_CELL = ("gene", "cell_0", "cell_1", "cell_2")
MESH = pl.DeviceIdType.MESH
F32 = jnp.float32
BF16 = jnp.bfloat16
LANES = (((1,), (1,)), ((), ()))

PAIR, ACROSS, DEEP, GACROSS, GDEEP = 0, 4, 20, 28, 44
PER_ROUND = 60
SPREAD = 2 * PER_ROUND
MESSAGES = SPREAD + PLANE


def hops(d):
    dy, dx = d // NX, d % NX
    return min(dy, NY - dy) + min(dx, NX - dx)


PLANE_ORDER = sorted(range(1, PLANE), key=lambda d: -hops(d))
Z_ORDER = sorted(range(1, NZ), key=lambda d: -min(d, NZ - d))


def split(value):
    high = value.astype(BF16)
    return high, (value - high.astype(F32)).astype(BF16)


def invert(packed):
    lane = lax.broadcasted_iota(jnp.int32, (8, 2 * K), 1)
    inner = lax.broadcasted_iota(jnp.int32, (8, 2 * K), 0)
    turned = pltpu.roll(packed, K, 1)
    parts = []
    for p in range(8):
        side = packed if p < 4 else turned
        at = 8 * (p % 4)
        eye = (lane == inner + (K + 8 * p)).astype(F32)
        parts.append(jnp.where(lane < K, side[at : at + 8], eye))
    out = []
    for p in range(8):
        block = parts[p]
        wide = [jnp.broadcast_to(block[:, 8 * p + j : 8 * p + j + 1], (8, 2 * K)) for j in range(8)]
        e = [[None] * 8 for _ in range(8)]
        for s in range(8):
            for j in range(s + 1):
                e[s][j] = jnp.broadcast_to(wide[j][s : s + 1, :], (8, 2 * K))
        rows = [jnp.broadcast_to(block[s : s + 1, :], (8, 2 * K)) for s in range(8)]
        lead = [
            [jnp.broadcast_to(parts[q][:, 8 * p + j : 8 * p + j + 1], (8, 2 * K)) for j in range(8)]
            for q in range(p + 1, 8)
        ]
        done = jnp.zeros((8, 2 * K), F32)
        for j in range(8):
            over = 1.0 / e[j][j]
            m = [e[s][j] * over for s in range(j + 1, 8)]
            for s in range(j + 1, 8):
                for t in range(j + 1, s + 1):
                    e[s][t] = e[s][t] - m[s - j - 1] * e[t][j]
            for s in range(j + 1, 8):
                rows[s] = rows[s] - m[s - j - 1] * rows[j]
            done = jnp.where(inner == j, rows[j] * lax.rsqrt(e[j][j]), done)
            for q in range(p + 1, 8):
                mine = lead[q - p - 1]
                for t in range(j + 1, 8):
                    mine[t] = mine[t] - mine[j] * m[t - j - 1]
                parts[q] = parts[q] - (mine[j] * over) * rows[j]
        out.append(done)
    return jnp.concatenate(out, axis=0)[:, K:]


def kernel(
    inverse_any, tiles_any, start_any, basis_ref, loadings_ref,
    inverse, tiles, x_ref, start, own, other, both, product, across, column, deep_in, pieces, pieces_in,
    gram, gacross, gdeep, lower_ref, mid, load_sem, send_sem, recv_sem,
):
    y, x, z = (lax.axis_index(name) for name in CELL)
    core = lax.axis_index("gene")
    other_core = 1 - core
    here = NX * y + x

    def in_plane(d):
        return (lax.rem(y + d // NX, NY), lax.rem(x + d % NX, NX), z, core)

    def on_z(d, which):
        return (y, x, lax.rem(z + d, NZ), which)

    partner = (y, x, z, other_core)
    loads = [
        pltpu.make_async_copy(tiles_any, tiles.at[pl.ds(0, SLOTS)], load_sem.at[0]),
        pltpu.make_async_copy(inverse_any, inverse, load_sem.at[1]),
        pltpu.make_async_copy(start_any, start, load_sem.at[2]),
    ]
    for load in loads:
        load.start()

    barrier = pltpu.get_barrier_semaphore()
    peers = [partner] + [in_plane(d) for d in range(1, PLANE)]
    peers += [on_z(d, core) for d in range(1, NZ)] + [on_z(d, other_core) for d in range(1, NZ)]
    for peer in peers:
        pl.semaphore_signal(barrier, inc=1, device_id=peer, device_id_type=MESH)

    tiles[SLOTS] = jnp.zeros((TILE, TILE), BF16)
    for load in loads:
        load.wait()
    pl.semaphore_wait(barrier, len(peers))

    def copy_of(src, dst, number, peer):
        return pltpu.make_async_remote_copy(
            src_ref=src, dst_ref=dst, send_sem=send_sem.at[number], recv_sem=recv_sem.at[number],
            device_id=peer, device_id_type=MESH,
        )

    def scores_into(r, basis_of):
        def pair_copy(i):
            return copy_of(own.at[r, i], other.at[r, i], r * PER_ROUND + PAIR + i, partner)

        def chunk(i, carry):
            at = pl.multiple_of(i * CHUNK, CHUNK)
            if r == 0:
                for k in range(2):
                    for c in range(COL_BLOCKS):
                        x_ref[pl.ds(pl.multiple_of(at + k * TILE, TILE), TILE), pl.ds(c * TILE, TILE)] = tiles[
                            inverse[(2 * i + k) * COL_BLOCKS + c]
                        ]
            own[r, i] = lax.dot_general(
                basis_of(), x_ref[pl.ds(at, CHUNK), :], LANES, preferred_element_type=F32
            )
            pair_copy(i).start()
            return carry

        lax.fori_loop(0, CHUNKS, chunk, 0)
        for i in range(CHUNKS):
            pair_copy(i).wait_recv()
            high, low = split(own[r, i] + other[r, i])
            both[:K, i * CHUNK : (i + 1) * CHUNK] = high
            both[K:, i * CHUNK : (i + 1) * CHUNK] = low

    def gram_across(r, d):
        return copy_of(gram.at[r], gacross.at[r, here], r * PER_ROUND + GACROSS + d, in_plane(d))

    def gram_deep(r, d, which):
        number = r * PER_ROUND + GDEEP + 8 * (1 - which) + d
        return copy_of(gdeep.at[r, z], gdeep.at[r, z], number, on_z(d, which))

    def gram_start(r):
        @pl.when(core == 1)
        def _():
            square = lax.dot_general(both[...], both[...], LANES, preferred_element_type=F32)
            square = square[:K] + square[K:]
            square = square + pltpu.roll(square, K, 1)
            half = lax.broadcasted_iota(jnp.int32, (K // 2, 2 * K), 1) < K
            packed = jnp.where(half, square[: K // 2], square[K // 2 :])
            gram[r] = packed
            gacross[r, here] = packed
            for d in PLANE_ORDER:
                gram_across(r, d).start()

    def gram_middle(r):
        @pl.when(core == 1)
        def _():
            for d in PLANE_ORDER:
                gram_across(r, d).wait_recv()
            total = gacross[r, 0]
            for n in range(1, PLANE):
                total = total + gacross[r, n]
            gdeep[r, z] = total
            for d in Z_ORDER:
                gram_deep(r, d, 1).start()
                gram_deep(r, d, 0).start()
            gram_deep(r, 0, 0).start()

    def gram_end(r):
        @pl.when(core == 1)
        def _():
            for d in Z_ORDER:
                gram_deep(r, d, 1).wait_recv()

        @pl.when(core == 0)
        def _():
            for d in range(NZ):
                gram_deep(r, d, 0).wait_recv()

        @pl.when(z >= 0)
        def _():
            total = gdeep[r, 0]
            for zz in range(1, NZ):
                total = total + gdeep[r, zz]
            high, low = split(invert(total))
            lower_ref[...] = jnp.concatenate([high, high, low, low], axis=1)

    def product_copy(r, n, d, peer):
        return copy_of(product.at[r, n], across.at[r, d], r * PER_ROUND + ACROSS + d, peer)

    def product_start(r):
        for dy in (2, 1, 3, 0):
            yy = lax.rem(y + dy, NY)

            def pair(i, carry):
                n = NX * yy + 2 * i
                doubled = jnp.dot(
                    both[...], x_ref[:, pl.ds(pl.multiple_of(n * TILE, 2 * TILE), 2 * TILE)],
                    preferred_element_type=F32,
                )
                summed = doubled[:K] + doubled[K:]
                for k in range(2):
                    product[r, n + k] = summed[:, k * TILE : (k + 1) * TILE]
                for k in range(2):
                    xx = 2 * i + k
                    d = NX * dy + lax.rem(xx - x + NX, NX)
                    copy = product_copy(r, n + k, d, (yy, xx, z, core))
                    if dy:
                        copy.start()
                    else:
                        pl.when(xx != x)(copy.start)
                return carry

            lax.fori_loop(0, 2, pair, 0)

    def product_middle(r):
        for d in PLANE_ORDER:
            product_copy(r, 0, d, in_plane(d)).wait_recv()
        total = product[r, here]
        for d in range(1, PLANE):
            total = total + across[r, d]
        return total

    scores_into(0, lambda: start[...])
    gram_start(0)
    product_start(0)
    gram_middle(0)
    deep_in[z] = product_middle(0)

    def whole_copy(d):
        return copy_of(deep_in.at[z], deep_in.at[z], DEEP + d, on_z(d, core))

    for d in Z_ORDER:
        whole_copy(d).start()
    gram_end(0)
    for d in Z_ORDER:
        whole_copy(d).wait_recv()
    total = deep_in[0]
    for zz in range(1, NZ):
        total = total + deep_in[zz]
    high, low = split(total)
    middle = jnp.dot(
        lower_ref[...], jnp.concatenate([high, low, high, low], axis=0), preferred_element_type=F32
    )
    mid[here] = middle.astype(BF16)

    def spread_copy(d):
        return copy_of(mid.at[here], mid.at[here], SPREAD + d, in_plane(d))

    for d in PLANE_ORDER:
        spread_copy(d).start()
    for d in PLANE_ORDER:
        spread_copy(d).wait_recv()

    scores_into(1, lambda: jnp.concatenate([mid[n] for n in range(PLANE)], axis=1))
    gram_start(1)
    product_start(1)
    gram_middle(1)
    block = product_middle(1)
    turned = jnp.transpose(jnp.concatenate([block, block], axis=0))
    lane_half = lax.broadcasted_iota(jnp.int32, (8, 2 * K), 1) < K
    for zz in range(NZ):
        pieces[zz] = jnp.where(lane_half, turned[16 * zz : 16 * zz + 8], turned[16 * zz + 8 : 16 * zz + 16])

    def piece_copy(d):
        peer = on_z(d, core)
        return copy_of(pieces.at[peer[2]], pieces_in.at[d], PER_ROUND + DEEP + d, peer)

    for d in Z_ORDER:
        piece_copy(d).start()
    gram_end(1)
    ortho = jnp.dot(
        lower_ref[...], jnp.concatenate([both[...], both[...]], axis=0), preferred_element_type=F32
    )
    basis_ref[...] = (ortho * jnp.sqrt(F32(TOTAL_CELLS))).astype(BF16)
    for d in Z_ORDER:
        piece_copy(d).wait_recv()
    piece = pieces[z]
    for d in range(1, NZ):
        piece = piece + pieces_in[d]
    high, low = split(jnp.concatenate([piece[:, :K], piece[:, K:]], axis=0))
    loadings_ref[...] = lax.dot_general(
        jnp.concatenate([high, low, high, low], axis=1), lower_ref[...], LANES, preferred_element_type=F32
    )

    for r in range(2):
        for i in range(CHUNKS):
            copy_of(own.at[r, i], other.at[r, i], r * PER_ROUND + PAIR + i, partner).wait_send()
        for d in PLANE_ORDER:
            product_copy(r, 0, d, in_plane(d)).wait_send()
    for d in Z_ORDER:
        whole_copy(d).wait_send()
        piece_copy(d).wait_send()
    for d in PLANE_ORDER:
        spread_copy(d).wait_send()

    @pl.when(core == 1)
    def _():
        for r in range(2):
            for d in PLANE_ORDER:
                gram_across(r, d).wait_send()
            for d in Z_ORDER:
                gram_deep(r, d, 1).wait_send()
            for d in range(NZ):
                gram_deep(r, d, 0).wait_send()


def local(tiles, tile_row, tile_col, tile_count, start_basis):
    places = ROW_BLOCKS * COL_BLOCKS
    slot = jnp.arange(SLOTS, dtype=jnp.int32)
    place = jnp.where(slot < tile_count[0, 0], tile_row[0] * COL_BLOCKS + tile_col[0], places)
    hit = place[None, :] == jnp.arange(places, dtype=jnp.int32)[:, None]
    inverse = jnp.min(jnp.where(hit, slot[None, :], SLOTS), axis=1)
    vmem = pl.BlockSpec(memory_space=pltpu.VMEM)
    anywhere = pl.BlockSpec(memory_space=pl.ANY)
    basis, loadings = pl.pallas_call(
        kernel,
        out_shape=(
            jax.ShapeDtypeStruct((K, CELLS), BF16),
            jax.ShapeDtypeStruct((GENES // (PLANE * NZ), K), F32),
        ),
        in_specs=[anywhere] * 3,
        out_specs=(vmem, vmem),
        scratch_shapes=[
            pltpu.SMEM((places,), jnp.int32),
            pltpu.VMEM((SLOTS + 1, TILE, TILE), BF16),
            pltpu.VMEM((CELLS, GENES), BF16),
            pltpu.VMEM((K, GENES), BF16),
            pltpu.VMEM((2, CHUNKS, K, CHUNK), F32),
            pltpu.VMEM((2, CHUNKS, K, CHUNK), F32),
            pltpu.VMEM((2 * K, CELLS), BF16),
            pltpu.VMEM((2, PLANE, K, TILE), F32),
            pltpu.VMEM((2, PLANE, K, TILE), F32),
            pltpu.VMEM((K, TILE), F32),
            pltpu.VMEM((NZ, K, TILE), F32),
            pltpu.VMEM((NZ, 8, TILE), F32),
            pltpu.VMEM((NZ, 8, TILE), F32),
            pltpu.VMEM((2, K // 2, 2 * K), F32),
            pltpu.VMEM((2, PLANE, K // 2, 2 * K), F32),
            pltpu.VMEM((2, NZ, K // 2, 2 * K), F32),
            pltpu.VMEM((K, 4 * K), BF16),
            pltpu.VMEM((PLANE, K, TILE), BF16),
            pltpu.SemaphoreType.DMA((3,)),
            pltpu.SemaphoreType.DMA((MESSAGES,)),
            pltpu.SemaphoreType.DMA((MESSAGES,)),
        ],
        compiler_params=pltpu.CompilerParams(collective_id=0, has_side_effects=True),
    )(inverse, tiles[0], start_basis)
    return basis, loadings.T


def solution(mesh):
    finer = Mesh(
        mesh.devices.reshape(NY, NX, NZ, mesh.shape["gene"]), ("cell_0", "cell_1", "cell_2", "gene")
    )
    return jax.shard_map(
        local,
        mesh=finer,
        in_specs=(
            P("gene", CELL, None, None),
            P("gene", CELL),
            P("gene", CELL),
            P("gene", CELL),
            P(None, "gene"),
        ),
        out_specs=(P(None, CELL), P(None, GENE_CELL)),
        check_vma=False,
    )
```

time: 261 us -> 67.2 us (0.26)
  the two profiles are of different devices: /device:TPU:32 before, /device:TPU:1 now
where the time goes in v2:
time: 67.2 us; the launch traced here: 67.1 us
  Pallas kernels  61.6 us (92%)
  local copies, waits for them, and re-layouts  2.86 us (4%)
  between operations  1.29 us (2%)
  other arithmetic  1.28 us (2%)
    pallas_call x1, Pallas kernels, local(): pl.pallas_call(kernel, out_shape=(jax.ShapeDtypeStruct((K, CELLS), BF16),...  61.6 us
    unnamed x2, local copies, waits for them, and re-layouts  2.86 us

profile of v2, /device:TPU:1, one launch (start us, length us, event | category | flops | bytes accessed | tf_op | source)
XLA Modules:
  0.0 67.1 jit_solution(4513849509000866712)
XLA Ops:
  1.3 0.7 %fusion = s32[64]{0:T(128)S(1)} fusion(s32[1,64]{1,0:T(1,128)} %param.7, s32[1,64]{1,0:T(1,128)} %param.6, s32[]{:T(128)} %bitcast.5), kind=kLoop, calls=%fused_computation.3 | loop fusion | flops 256 | bytes 772 | tf_op jit(solution)/shard_map/eq | solution.py:335
  2.0 0.6 select_reduce_fusion.inverse_any
  2.6 61.6 %shard_map.68 = (bf16[64,1024]{1,0:T(8,128)(2,1)}, f32[16,64]{1,0:T(8,128)}) custom-call(s32[128]{0:T(128)} %select_reduce_fusion.inverse_any, bf16[64,128,128]{2,1,0:T(8,128)(2,1)} %bitcast.6, bf16[64,2048]{1,0:T(8,128)(2,1)} %start_any.1), custom_call_target="tpu_custom_call" | custom-call | tf_op jit(solution)/shard_map/pallas_call | solution.py:339
  64.2 1.6 %copy.10 = bf16[64,1024]{1,0:T(8,128)(2,1)} copy(bf16[64,1024]{1,0:T(8,128)(2,1)} %get-tuple-element.8) | data formatting | bytes 262144
  65.8 1.3 %copy.11 = f32[64,16]{0,1:T(8,128)} copy(f32[64,16]{0,1:T(8,128)} %bitcast.7) | data formatting | bytes 8192

commit v3 on v2

--- a/solution.py
+++ b/solution.py
@@ -15,7 +15,7 @@
 GENES = COL_BLOCKS * TILE
 NY, NX, NZ = 4, 4, 8
 PLANE = NY * NX
-CHUNKS = 4
+CHUNKS = 2
 CHUNK = CELLS // CHUNKS
 PAIRS = COL_BLOCKS // 2
 TOTAL_CELLS = PLANE * NZ * CELLS
@@ -88,10 +88,22 @@
     return jnp.concatenate(out, axis=0)[:, K:]
 
 
+def finish(lower_ref, both_ref, piece_ref, basis_ref, loadings_ref):
+    ortho = jnp.dot(
+        lower_ref[...], jnp.concatenate([both_ref[...], both_ref[...]], axis=0), preferred_element_type=F32
+    )
+    basis_ref[...] = (ortho * jnp.sqrt(F32(TOTAL_CELLS))).astype(BF16)
+    piece = piece_ref[...]
+    high, low = split(jnp.concatenate([piece[:, :K], piece[:, K:]], axis=0))
+    loadings_ref[...] = lax.dot_general(
+        jnp.concatenate([high, low, high, low], axis=1), lower_ref[...], LANES, preferred_element_type=F32
+    )
+
+
 def kernel(
-    inverse_any, tiles_any, start_any, basis_ref, loadings_ref,
-    inverse, tiles, x_ref, start, own, other, both, product, across, column, deep_in, pieces, pieces_in,
-    gram, gacross, gdeep, lower_ref, mid, load_sem, send_sem, recv_sem,
+    row_any, col_any, count_any, tiles_any, start_any, lower_ref, both, piece_ref,
+    places, count, inverse_v, inverse, tiles, x_ref, start, own, other, product, across, deep_in, pieces, pieces_in,
+    gram, gacross, gdeep, mid, partial, load_sem, send_sem, recv_sem,
 ):
     y, x, z = (lax.axis_index(name) for name in CELL)
     core = lax.axis_index("gene")
@@ -106,9 +118,11 @@
 
     partner = (y, x, z, other_core)
     loads = [
-        pltpu.make_async_copy(tiles_any, tiles.at[pl.ds(0, SLOTS)], load_sem.at[0]),
-        pltpu.make_async_copy(inverse_any, inverse, load_sem.at[1]),
-        pltpu.make_async_copy(start_any, start, load_sem.at[2]),
+        pltpu.make_async_copy(row_any, places.at[0], load_sem.at[0]),
+        pltpu.make_async_copy(col_any, places.at[1], load_sem.at[1]),
+        pltpu.make_async_copy(count_any, count, load_sem.at[2]),
+        pltpu.make_async_copy(tiles_any, tiles.at[pl.ds(0, SLOTS)], load_sem.at[3]),
+        pltpu.make_async_copy(start_any, start, load_sem.at[4]),
     ]
     for load in loads:
         load.start()
@@ -120,9 +134,19 @@
         pl.semaphore_signal(barrier, inc=1, device_id=peer, device_id_type=MESH)
 
     tiles[SLOTS] = jnp.zeros((TILE, TILE), BF16)
-    for load in loads:
+    for load in loads[:3]:
         load.wait()
-    pl.semaphore_wait(barrier, len(peers))
+    lane = lax.broadcasted_iota(jnp.int32, (1, SLOTS), 1)
+    place = jnp.where(lane < count[...], places[0] * COL_BLOCKS + places[1], ROW_BLOCKS * COL_BLOCKS)
+    turned = jnp.transpose(jnp.broadcast_to(jnp.concatenate([place, place], axis=1), (TILE, TILE)))[:SLOTS]
+    slot = lax.broadcasted_iota(jnp.int32, (SLOTS, TILE), 0)
+    spot = lax.broadcasted_iota(jnp.int32, (SLOTS, TILE), 1)
+    inverse_v[...] = jnp.min(jnp.where(turned == spot, slot, SLOTS), axis=0, keepdims=True)
+    lookup = pltpu.make_async_copy(inverse_v, inverse, load_sem.at[5])
+    lookup.start()
+    for load in loads[3:]:
+        load.wait()
+    lookup.wait()
 
     def copy_of(src, dst, number, peer):
         return pltpu.make_async_remote_copy(
@@ -130,27 +154,33 @@
             device_id=peer, device_id_type=MESH,
         )
 
-    def scores_into(r, basis_of):
-        def pair_copy(i):
-            return copy_of(own.at[r, i], other.at[r, i], r * PER_ROUND + PAIR + i, partner)
-
-        def chunk(i, carry):
-            at = pl.multiple_of(i * CHUNK, CHUNK)
-            if r == 0:
-                for k in range(2):
-                    for c in range(COL_BLOCKS):
-                        x_ref[pl.ds(pl.multiple_of(at + k * TILE, TILE), TILE), pl.ds(c * TILE, TILE)] = tiles[
-                            inverse[(2 * i + k) * COL_BLOCKS + c]
-                        ]
-            own[r, i] = lax.dot_general(
-                basis_of(), x_ref[pl.ds(at, CHUNK), :], LANES, preferred_element_type=F32
-            )
-            pair_copy(i).start()
-            return carry
-
-        lax.fori_loop(0, CHUNKS, chunk, 0)
+    def pair_copy(r, i):
+        return copy_of(own.at[r, i], other.at[r, i], r * PER_ROUND + PAIR + i, partner)
+
+    def build(i):
+        for k in range(CHUNK // TILE):
+            row = i * CHUNK + k * TILE
+            for c in range(COL_BLOCKS):
+                x_ref[c, row : row + TILE] = tiles[inverse[0, row // TILE * COL_BLOCKS + c]]
+
+    def cells_of(i, columns):
+        return jnp.concatenate([x_ref[n, i * CHUNK : (i + 1) * CHUNK] for n in columns], axis=1)
+
+    def chunk(r, i, scores_of):
+        @pl.when(z >= 0)
+        def _():
+            if r == 0 and i == 1:
+                pl.semaphore_wait(barrier, len(peers))
+            if i > 0:
+                pair_copy(r, i - 1).start()
+            if r == 0 and i + 1 < CHUNKS:
+                build(i + 1)
+            own[r, i] = scores_of(i)
+
+    def join(r):
+        pair_copy(r, CHUNKS - 1).start()
         for i in range(CHUNKS):
-            pair_copy(i).wait_recv()
+            pair_copy(r, i).wait_recv()
             high, low = split(own[r, i] + other[r, i])
             both[:K, i * CHUNK : (i + 1) * CHUNK] = high
             both[K:, i * CHUNK : (i + 1) * CHUNK] = low
@@ -215,26 +245,19 @@
         for dy in (2, 1, 3, 0):
             yy = lax.rem(y + dy, NY)
 
-            def pair(i, carry):
-                n = NX * yy + 2 * i
+            @pl.when(z >= 0)
+            def _():
+                n = NX * yy
                 doubled = jnp.dot(
-                    both[...], x_ref[:, pl.ds(pl.multiple_of(n * TILE, 2 * TILE), 2 * TILE)],
-                    preferred_element_type=F32,
+                    both[...], jnp.concatenate([x_ref[n + k] for k in range(NX)], axis=1), preferred_element_type=F32
                 )
                 summed = doubled[:K] + doubled[K:]
-                for k in range(2):
+                for k in range(NX):
                     product[r, n + k] = summed[:, k * TILE : (k + 1) * TILE]
-                for k in range(2):
-                    xx = 2 * i + k
-                    d = NX * dy + lax.rem(xx - x + NX, NX)
-                    copy = product_copy(r, n + k, d, (yy, xx, z, core))
-                    if dy:
-                        copy.start()
-                    else:
-                        pl.when(xx != x)(copy.start)
-                return carry
-
-            lax.fori_loop(0, 2, pair, 0)
+                for dx in (2, 1, 3, 0):
+                    if dy or dx:
+                        xx = lax.rem(x + dx, NX)
+                        product_copy(r, n + xx, NX * dy + dx, (yy, xx, z, core)).start()
 
     def product_middle(r):
         for d in PLANE_ORDER:
@@ -244,7 +267,14 @@
             total = total + across[r, d]
         return total
 
-    scores_into(0, lambda: start[...])
+    build(0)
+    for i in range(CHUNKS):
+        chunk(
+            0, i, lambda i: lax.dot_general(
+                start[...], cells_of(i, range(COL_BLOCKS)), LANES, preferred_element_type=F32
+            ),
+        )
+    join(0)
     gram_start(0)
     product_start(0)
     gram_middle(0)
@@ -272,10 +302,26 @@
 
     for d in PLANE_ORDER:
         spread_copy(d).start()
-    for d in PLANE_ORDER:
+    def scores_with(i, offsets):
+        at = [NX * lax.rem(y + NY - d // NX, NY) + lax.rem(x + NX - d % NX, NX) for d in offsets]
+        return lax.dot_general(
+            jnp.concatenate([mid[n] for n in at], axis=1),
+            cells_of(i, at), LANES, preferred_element_type=F32,
+        )
+
+    near, far = [0] + PLANE_ORDER[:3:-1], PLANE_ORDER[:4]
+    for d in near[1:]:
         spread_copy(d).wait_recv()
-
-    scores_into(1, lambda: jnp.concatenate([mid[n] for n in range(PLANE)], axis=1))
+    for i in range(CHUNKS):
+        @pl.when(z >= 0)
+        def _():
+            partial[i] = scores_with(i, near)
+
+    for d in far:
+        spread_copy(d).wait_recv()
+    for i in range(CHUNKS):
+        chunk(1, i, lambda i: partial[i] + scores_with(i, far))
+    join(1)
     gram_start(1)
     product_start(1)
     gram_middle(1)
@@ -292,23 +338,16 @@
     for d in Z_ORDER:
         piece_copy(d).start()
     gram_end(1)
-    ortho = jnp.dot(
-        lower_ref[...], jnp.concatenate([both[...], both[...]], axis=0), preferred_element_type=F32
-    )
-    basis_ref[...] = (ortho * jnp.sqrt(F32(TOTAL_CELLS))).astype(BF16)
     for d in Z_ORDER:
         piece_copy(d).wait_recv()
     piece = pieces[z]
     for d in range(1, NZ):
         piece = piece + pieces_in[d]
-    high, low = split(jnp.concatenate([piece[:, :K], piece[:, K:]], axis=0))
-    loadings_ref[...] = lax.dot_general(
-        jnp.concatenate([high, low, high, low], axis=1), lower_ref[...], LANES, preferred_element_type=F32
-    )
+    piece_ref[...] = piece
 
     for r in range(2):
         for i in range(CHUNKS):
-            copy_of(own.at[r, i], other.at[r, i], r * PER_ROUND + PAIR + i, partner).wait_send()
+            pair_copy(r, i).wait_send()
         for d in PLANE_ORDER:
             product_copy(r, 0, d, in_plane(d)).wait_send()
     for d in Z_ORDER:
@@ -329,46 +368,52 @@
 
 
 def local(tiles, tile_row, tile_col, tile_count, start_basis):
-    places = ROW_BLOCKS * COL_BLOCKS
-    slot = jnp.arange(SLOTS, dtype=jnp.int32)
-    place = jnp.where(slot < tile_count[0, 0], tile_row[0] * COL_BLOCKS + tile_col[0], places)
-    hit = place[None, :] == jnp.arange(places, dtype=jnp.int32)[:, None]
-    inverse = jnp.min(jnp.where(hit, slot[None, :], SLOTS), axis=1)
     vmem = pl.BlockSpec(memory_space=pltpu.VMEM)
-    anywhere = pl.BlockSpec(memory_space=pl.ANY)
-    basis, loadings = pl.pallas_call(
+    anywhere = pl.BlockSpec(memory_space=pltpu.HBM)
+    parts = pl.pallas_call(
         kernel,
         out_shape=(
-            jax.ShapeDtypeStruct((K, CELLS), BF16),
-            jax.ShapeDtypeStruct((GENES // (PLANE * NZ), K), F32),
+            pltpu.VMEM((K, 4 * K), BF16),
+            pltpu.VMEM((2 * K, CELLS), BF16),
+            pltpu.VMEM((8, TILE), F32),
         ),
-        in_specs=[anywhere] * 3,
-        out_specs=(vmem, vmem),
+        in_specs=[anywhere] * 5,
+        out_specs=(vmem, vmem, vmem),
         scratch_shapes=[
-            pltpu.SMEM((places,), jnp.int32),
+            pltpu.VMEM((2, 1, SLOTS), jnp.int32),
+            pltpu.VMEM((1, 1), jnp.int32),
+            pltpu.VMEM((1, ROW_BLOCKS * COL_BLOCKS), jnp.int32),
+            pltpu.SMEM((1, ROW_BLOCKS * COL_BLOCKS), jnp.int32),
             pltpu.VMEM((SLOTS + 1, TILE, TILE), BF16),
-            pltpu.VMEM((CELLS, GENES), BF16),
+            pltpu.VMEM((COL_BLOCKS, CELLS, TILE), BF16),
             pltpu.VMEM((K, GENES), BF16),
             pltpu.VMEM((2, CHUNKS, K, CHUNK), F32),
             pltpu.VMEM((2, CHUNKS, K, CHUNK), F32),
-            pltpu.VMEM((2 * K, CELLS), BF16),
             pltpu.VMEM((2, PLANE, K, TILE), F32),
             pltpu.VMEM((2, PLANE, K, TILE), F32),
-            pltpu.VMEM((K, TILE), F32),
             pltpu.VMEM((NZ, K, TILE), F32),
             pltpu.VMEM((NZ, 8, TILE), F32),
             pltpu.VMEM((NZ, 8, TILE), F32),
             pltpu.VMEM((2, K // 2, 2 * K), F32),
             pltpu.VMEM((2, PLANE, K // 2, 2 * K), F32),
             pltpu.VMEM((2, NZ, K // 2, 2 * K), F32),
-            pltpu.VMEM((K, 4 * K), BF16),
             pltpu.VMEM((PLANE, K, TILE), BF16),
-            pltpu.SemaphoreType.DMA((3,)),
+            pltpu.VMEM((CHUNKS, K, CHUNK), F32),
+            pltpu.SemaphoreType.DMA((6,)),
             pltpu.SemaphoreType.DMA((MESSAGES,)),
             pltpu.SemaphoreType.DMA((MESSAGES,)),
         ],
         compiler_params=pltpu.CompilerParams(collective_id=0, has_side_effects=True),
-    )(inverse, tiles[0], start_basis)
+    )(tile_row, tile_col, tile_count, tiles[0], start_basis)
+    basis, loadings = pl.pallas_call(
+        finish,
+        out_shape=(
+            jax.ShapeDtypeStruct((K, CELLS), BF16),
+            jax.ShapeDtypeStruct((GENES // (PLANE * NZ), K), F32),
+        ),
+        in_specs=[vmem] * 3,
+        out_specs=(vmem, vmem),
+    )(*(pltpu.with_memory_space_constraint(part, pltpu.VMEM) for part in parts))
     return basis, loadings.T
 
 

time: 67.2 us -> 60 us (0.89)
  Pallas kernels: 61.6 us -> 58.6 us
  local copies, waits for them, and re-layouts: 2.86 us -> 0 us
  other arithmetic: 1.28 us -> 0 us
    pallas_call x1 -> x2, Pallas kernels: 61.6 us -> 58.6 us  [the longest x1 57.7 us: local(): pl.pallas_call(kernel, out_shape=(pltpu.VMEM((K, 4 * K), BF16), pltpu.VME...]
    unnamed x2 -> x0, local copies, waits for them, and re-layouts: 2.86 us -> none
    eq x1 -> x0, other arithmetic: 0.68 us -> none  [local(): hit = place[None, :] == jnp.arange(places, dtype=jnp.int32)[:, None]]
where the time goes in v3:
time: 60 us; the launch traced here: 59.9 us
  Pallas kernels  58.6 us (98%)
  between operations  1.29 us (2%)
    pallas_call x1, Pallas kernels, local(): pl.pallas_call(kernel, out_shape=(pltpu.VMEM((K, 4 * K), BF16), pltpu.VME...  57.7 us

profile of v3, /device:TPU:1, one launch (start us, length us, event | category | flops | bytes accessed | tf_op | source)
XLA Modules:
  0.0 59.9 jit_solution(14831632982578986731)
XLA Ops:
  1.3 57.7 %shard_map.68 = (bf16[64,256]{1,0:T(8,128)(2,1)S(1)}, bf16[128,1024]{1,0:T(8,128)(2,1)S(1)}, f32[8,128]{1,0:T(8,128)S(1)}) custom-call(s32[1,64]{1,0:T(1,128)} %row_any.1, s32[1,64]{1,0:T(1,128)} %col_any.1, s32[1,1]{1,0:T(1,128)S(6)} %copy.7.count_any, bf16[64,128,128]{2,1,0:T(8,128)(2,1)} %bitcast.2, bf16[64,2048]{1,0:T(8,128)(2,1)} %start_any.1), custom_call_target="tpu_custom_call" | custom-call | tf_op jit(solution)/shard_map/pallas_call | solution.py:373
  59.0 0.9 %shard_map.69 = (bf16[64,1024]{1,0:T(8,128)(2,1)}, f32[16,64]{1,0:T(8,128)}) custom-call(bf16[64,256]{1,0:T(8,128)(2,1)S(1)} %get-tuple-element.7.lower_ref, bf16[128,1024]{1,0:T(8,128)(2,1)S(1)} %get-tuple-element.8.both_ref, f32[8,128]{1,0:T(8,128)S(1)} %get-tuple-element.9.piece_ref), custom_call_target="tpu_custom_call" | custom-call | tf_op jit(solution)/shard_map/pallas_call | solution.py:408

commit v4 on v3

--- a/solution.py
+++ b/solution.py
@@ -26,8 +26,10 @@
 BF16 = jnp.bfloat16
 LANES = (((1,), (1,)), ((), ()))
 
-PAIR, ACROSS, DEEP, GACROSS, GDEEP = 0, 4, 20, 28, 44
-PER_ROUND = 60
+PAIR, ACROSS, DEEP, GACROSS, GDEEP = 0, 2, 34, 50, 66
+PER_ROUND = 82
+LOADS = 8
+HALVES = (2, 1)
 SPREAD = 2 * PER_ROUND
 MESSAGES = SPREAD + PLANE
 
@@ -44,6 +46,10 @@
 def split(value):
     high = value.astype(BF16)
     return high, (value - high.astype(F32)).astype(BF16)
+
+
+def spread_lane(value, at):
+    return jnp.take_along_axis(value, jnp.full(value.shape, at, jnp.int32), axis=1)
 
 
 def invert(packed):
@@ -59,14 +65,14 @@
     out = []
     for p in range(8):
         block = parts[p]
-        wide = [jnp.broadcast_to(block[:, 8 * p + j : 8 * p + j + 1], (8, 2 * K)) for j in range(8)]
+        wide = [spread_lane(block, 8 * p + j) for j in range(8)]
         e = [[None] * 8 for _ in range(8)]
         for s in range(8):
             for j in range(s + 1):
                 e[s][j] = jnp.broadcast_to(wide[j][s : s + 1, :], (8, 2 * K))
         rows = [jnp.broadcast_to(block[s : s + 1, :], (8, 2 * K)) for s in range(8)]
         lead = [
-            [jnp.broadcast_to(parts[q][:, 8 * p + j : 8 * p + j + 1], (8, 2 * K)) for j in range(8)]
+            [spread_lane(parts[q], 8 * p + j) for j in range(8)]
             for q in range(p + 1, 8)
         ]
         done = jnp.zeros((8, 2 * K), F32)
@@ -121,9 +127,11 @@
         pltpu.make_async_copy(row_any, places.at[0], load_sem.at[0]),
         pltpu.make_async_copy(col_any, places.at[1], load_sem.at[1]),
         pltpu.make_async_copy(count_any, count, load_sem.at[2]),
-        pltpu.make_async_copy(tiles_any, tiles.at[pl.ds(0, SLOTS)], load_sem.at[3]),
-        pltpu.make_async_copy(start_any, start, load_sem.at[4]),
+        pltpu.make_async_copy(start_any, start, load_sem.at[3]),
     ]
+    for n in range(LOADS):
+        rows = pl.ds(n * SLOTS // LOADS, SLOTS // LOADS)
+        loads.append(pltpu.make_async_copy(tiles_any.at[rows], tiles.at[rows], load_sem.at[5 + n]))
     for load in loads:
         load.start()
 
@@ -142,7 +150,7 @@
     slot = lax.broadcasted_iota(jnp.int32, (SLOTS, TILE), 0)
     spot = lax.broadcasted_iota(jnp.int32, (SLOTS, TILE), 1)
     inverse_v[...] = jnp.min(jnp.where(turned == spot, slot, SLOTS), axis=0, keepdims=True)
-    lookup = pltpu.make_async_copy(inverse_v, inverse, load_sem.at[5])
+    lookup = pltpu.make_async_copy(inverse_v, inverse, load_sem.at[4])
     lookup.start()
     for load in loads[3:]:
         load.wait()
@@ -238,16 +246,22 @@
             high, low = split(invert(total))
             lower_ref[...] = jnp.concatenate([high, high, low, low], axis=1)
 
-    def product_copy(r, n, d, peer):
-        return copy_of(product.at[r, n], across.at[r, d], r * PER_ROUND + ACROSS + d, peer)
+    def product_copy(r, h, n, d, peer):
+        rows = pl.ds(h * K // HALVES[r], K // HALVES[r])
+        number = r * PER_ROUND + ACROSS + PLANE * h + d
+        return copy_of(product.at[r, n, rows], across.at[r, d, rows], number, peer)
 
     def product_start(r):
+        def send(h, dy, dx):
+            if dy or dx:
+                yy, xx = lax.rem(y + dy, NY), lax.rem(x + dx, NX)
+                product_copy(r, h, NX * yy + xx, NX * dy + dx, (yy, xx, z, core)).start()
+
         for dy in (2, 1, 3, 0):
-            yy = lax.rem(y + dy, NY)
+            n = NX * lax.rem(y + dy, NY)
 
             @pl.when(z >= 0)
             def _():
-                n = NX * yy
                 doubled = jnp.dot(
                     both[...], jnp.concatenate([x_ref[n + k] for k in range(NX)], axis=1), preferred_element_type=F32
                 )
@@ -255,17 +269,37 @@
                 for k in range(NX):
                     product[r, n + k] = summed[:, k * TILE : (k + 1) * TILE]
                 for dx in (2, 1, 3, 0):
-                    if dy or dx:
-                        xx = lax.rem(x + dx, NX)
-                        product_copy(r, n + xx, NX * dy + dx, (yy, xx, z, core)).start()
-
-    def product_middle(r):
+                    send(0, dy, dx)
+
+        for h in range(1, HALVES[r]):
+            for dy in (2, 1, 3, 0):
+                for dx in (2, 1, 3, 0):
+                    send(h, dy, dx)
+
+    def product_middle(r, h):
         for d in PLANE_ORDER:
-            product_copy(r, 0, d, in_plane(d)).wait_recv()
-        total = product[r, here]
+            product_copy(r, h, 0, d, in_plane(d)).wait_recv()
+        rows = slice(h * K // HALVES[r], (h + 1) * K // HALVES[r])
+        total = product[r, here, rows]
         for d in range(1, PLANE):
-            total = total + across[r, d]
+            total = total + across[r, d, rows]
         return total
+
+    def left(r):
+        for i in range(CHUNKS):
+            pair_copy(r, i).wait_send()
+        for h in range(HALVES[r]):
+            for d in PLANE_ORDER:
+                product_copy(r, h, 0, d, in_plane(d)).wait_send()
+
+        @pl.when(core == 1)
+        def _():
+            for d in PLANE_ORDER:
+                gram_across(r, d).wait_send()
+            for d in Z_ORDER:
+                gram_deep(r, d, 1).wait_send()
+            for d in range(NZ):
+                gram_deep(r, d, 0).wait_send()
 
     build(0)
     for i in range(CHUNKS):
@@ -278,16 +312,18 @@
     gram_start(0)
     product_start(0)
     gram_middle(0)
-    deep_in[z] = product_middle(0)
-
-    def whole_copy(d):
-        return copy_of(deep_in.at[z], deep_in.at[z], DEEP + d, on_z(d, core))
-
-    for d in Z_ORDER:
-        whole_copy(d).start()
+    def whole_copy(h, d):
+        rows = pl.ds(h * K // HALVES[0], K // HALVES[0])
+        return copy_of(deep_in.at[z, rows], deep_in.at[z, rows], DEEP + NZ * h + d, on_z(d, core))
+
+    for h in range(HALVES[0]):
+        deep_in[z, h * K // HALVES[0] : (h + 1) * K // HALVES[0]] = product_middle(0, h)
+        for d in Z_ORDER:
+            whole_copy(h, d).start()
     gram_end(0)
-    for d in Z_ORDER:
-        whole_copy(d).wait_recv()
+    for h in range(HALVES[0]):
+        for d in Z_ORDER:
+            whole_copy(h, d).wait_recv()
     total = deep_in[0]
     for zz in range(1, NZ):
         total = total + deep_in[zz]
@@ -324,8 +360,14 @@
     join(1)
     gram_start(1)
     product_start(1)
+    left(0)
+    for h in range(HALVES[0]):
+        for d in Z_ORDER:
+            whole_copy(h, d).wait_send()
+    for d in PLANE_ORDER:
+        spread_copy(d).wait_send()
     gram_middle(1)
-    block = product_middle(1)
+    block = product_middle(1, 0)
     turned = jnp.transpose(jnp.concatenate([block, block], axis=0))
     lane_half = lax.broadcasted_iota(jnp.int32, (8, 2 * K), 1) < K
     for zz in range(NZ):
@@ -345,26 +387,9 @@
         piece = piece + pieces_in[d]
     piece_ref[...] = piece
 
-    for r in range(2):
-        for i in range(CHUNKS):
-            pair_copy(r, i).wait_send()
-        for d in PLANE_ORDER:
-            product_copy(r, 0, d, in_plane(d)).wait_send()
+    left(1)
     for d in Z_ORDER:
-        whole_copy(d).wait_send()
         piece_copy(d).wait_send()
-    for d in PLANE_ORDER:
-        spread_copy(d).wait_send()
-
-    @pl.when(core == 1)
-    def _():
-        for r in range(2):
-            for d in PLANE_ORDER:
-                gram_across(r, d).wait_send()
-            for d in Z_ORDER:
-                gram_deep(r, d, 1).wait_send()
-            for d in range(NZ):
-                gram_deep(r, d, 0).wait_send()
 
 
 def local(tiles, tile_row, tile_col, tile_count, start_basis):
@@ -399,7 +424,7 @@
             pltpu.VMEM((2, NZ, K // 2, 2 * K), F32),
             pltpu.VMEM((PLANE, K, TILE), BF16),
             pltpu.VMEM((CHUNKS, K, CHUNK), F32),
-            pltpu.SemaphoreType.DMA((6,)),
+            pltpu.SemaphoreType.DMA((5 + LOADS,)),
             pltpu.SemaphoreType.DMA((MESSAGES,)),
             pltpu.SemaphoreType.DMA((MESSAGES,)),
         ],

time: 60 us -> 60.3 us (level)
  no operation moved by 1% of the time
where the time goes in v4:
time: 60.3 us; the launch traced here: 60.2 us
  Pallas kernels  58.9 us (98%)
  between operations  1.29 us (2%)
    pallas_call x1, Pallas kernels, local(): pl.pallas_call(kernel, out_shape=(pltpu.VMEM((K, 4 * K), BF16), pltpu.VME...  58 us

profile of v4, /device:TPU:1, one launch (start us, length us, event | category | flops | bytes accessed | tf_op | source)
XLA Modules:
  0.0 60.2 jit_solution(4831279398521708762)
XLA Ops:
  1.3 58.0 %shard_map.68 = (bf16[64,256]{1,0:T(8,128)(2,1)S(1)}, bf16[128,1024]{1,0:T(8,128)(2,1)S(1)}, f32[8,128]{1,0:T(8,128)S(1)}) custom-call(s32[1,64]{1,0:T(1,128)} %row_any.1, s32[1,64]{1,0:T(1,128)} %col_any.1, s32[1,1]{1,0:T(1,128)S(6)} %copy.7.count_any, bf16[64,128,128]{2,1,0:T(8,128)(2,1)} %bitcast.2, bf16[64,2048]{1,0:T(8,128)(2,1)} %start_any.1), custom_call_target="tpu_custom_call" | custom-call | tf_op jit(solution)/shard_map/pallas_call | solution.py:398
  59.3 0.9 %shard_map.69 = (bf16[64,1024]{1,0:T(8,128)(2,1)}, f32[16,64]{1,0:T(8,128)}) custom-call(bf16[64,256]{1,0:T(8,128)(2,1)S(1)} %get-tuple-element.7.lower_ref, bf16[128,1024]{1,0:T(8,128)(2,1)S(1)} %get-tuple-element.8.both_ref, f32[8,128]{1,0:T(8,128)S(1)} %get-tuple-element.9.piece_ref), custom_call_target="tpu_custom_call" | custom-call | tf_op jit(solution)/shard_map/pallas_call | solution.py:433

commit v5 on v4

--- a/solution.py
+++ b/solution.py
@@ -28,7 +28,7 @@
 
 PAIR, ACROSS, DEEP, GACROSS, GDEEP = 0, 2, 34, 50, 66
 PER_ROUND = 82
-LOADS = 8
+LOADS = 1
 HALVES = (2, 1)
 SPREAD = 2 * PER_ROUND
 MESSAGES = SPREAD + PLANE
@@ -49,7 +49,7 @@
 
 
 def spread_lane(value, at):
-    return jnp.take_along_axis(value, jnp.full(value.shape, at, jnp.int32), axis=1)
+    return jnp.broadcast_to(value[:, at : at + 1], value.shape)
 
 
 def invert(packed):
@@ -269,7 +269,12 @@
                 for k in range(NX):
                     product[r, n + k] = summed[:, k * TILE : (k + 1) * TILE]
                 for dx in (2, 1, 3, 0):
-                    send(0, dy, dx)
+                    pl.when(core >= r)(lambda dy=dy, dx=dx: send(0, dy, dx))
+
+        @pl.when(core < r)
+        def _():
+            for d in PLANE_ORDER:
+                send(0, d // NX, d % NX)
 
         for h in range(1, HALVES[r]):
             for dy in (2, 1, 3, 0):
@@ -360,12 +365,6 @@
     join(1)
     gram_start(1)
     product_start(1)
-    left(0)
-    for h in range(HALVES[0]):
-        for d in Z_ORDER:
-            whole_copy(h, d).wait_send()
-    for d in PLANE_ORDER:
-        spread_copy(d).wait_send()
     gram_middle(1)
     block = product_middle(1, 0)
     turned = jnp.transpose(jnp.concatenate([block, block], axis=0))
@@ -387,6 +386,12 @@
         piece = piece + pieces_in[d]
     piece_ref[...] = piece
 
+    left(0)
+    for h in range(HALVES[0]):
+        for d in Z_ORDER:
+            whole_copy(h, d).wait_send()
+    for d in PLANE_ORDER:
+        spread_copy(d).wait_send()
     left(1)
     for d in Z_ORDER:
         piece_copy(d).wait_send()

time: 60.3 us -> 58.1 us (0.964)
  Pallas kernels: 58.9 us -> 56.7 us
    pallas_call x1, Pallas kernels: 58 us -> 55.8 us  [local(): pl.pallas_call(kernel, out_shape=(pltpu.VMEM((K, 4 * K), BF16), pltpu.VME...]
where the time goes in v5:
time: 58.1 us; the launch traced here: 58 us
  Pallas kernels  56.7 us (98%)
  between operations  1.29 us (2%)
    pallas_call x1, Pallas kernels, local(): pl.pallas_call(kernel, out_shape=(pltpu.VMEM((K, 4 * K), BF16), pltpu.VME...  55.8 us

profile of v5, /device:TPU:1, one launch (start us, length us, event | category | flops | bytes accessed | tf_op | source)
XLA Modules:
  0.0 58.0 jit_solution(6056605726831644651)
XLA Ops:
  1.3 55.8 %shard_map.68 = (bf16[64,256]{1,0:T(8,128)(2,1)S(1)}, bf16[128,1024]{1,0:T(8,128)(2,1)S(1)}, f32[8,128]{1,0:T(8,128)S(1)}) custom-call(s32[1,64]{1,0:T(1,128)} %row_any.1, s32[1,64]{1,0:T(1,128)} %col_any.1, s32[1,1]{1,0:T(1,128)S(6)} %copy.7.count_any, bf16[64,128,128]{2,1,0:T(8,128)(2,1)} %bitcast.2, bf16[64,2048]{1,0:T(8,128)(2,1)} %start_any.1), custom_call_target="tpu_custom_call" | custom-call | tf_op jit(solution)/shard_map/pallas_call | solution.py:403
  57.1 0.9 %shard_map.69 = (bf16[64,1024]{1,0:T(8,128)(2,1)}, f32[16,64]{1,0:T(8,128)}) custom-call(bf16[64,256]{1,0:T(8,128)(2,1)S(1)} %get-tuple-element.7.lower_ref, bf16[128,1024]{1,0:T(8,128)(2,1)S(1)} %get-tuple-element.8.both_ref, f32[8,128]{1,0:T(8,128)S(1)} %get-tuple-element.9.piece_ref), custom_call_target="tpu_custom_call" | custom-call | tf_op jit(solution)/shard_map/pallas_call | solution.py:438

commit v6 on v5

--- a/solution.py
+++ b/solution.py
@@ -52,16 +52,36 @@
     return jnp.broadcast_to(value[:, at : at + 1], value.shape)
 
 
+def pack(twice):
+    quarter = lax.broadcasted_iota(jnp.int32, (8, 2 * K), 1) // 32
+    ahead, back = pltpu.roll(twice, 32, 1), pltpu.roll(twice, 96, 1)
+
+    def joined(row, sources):
+        value = sources[0][row : row + 8]
+        for k in range(1, 4):
+            value = jnp.where(quarter == k, sources[k][row + 8 * k : row + 8 * k + 8], value)
+        return value
+
+    return jnp.concatenate(
+        [joined(0, (twice, ahead) * 2), joined(32, (twice, ahead) * 2), joined(32, (back, twice) * 2)], axis=0
+    )
+
+
 def invert(packed):
     lane = lax.broadcasted_iota(jnp.int32, (8, 2 * K), 1)
     inner = lax.broadcasted_iota(jnp.int32, (8, 2 * K), 0)
-    turned = pltpu.roll(packed, K, 1)
+
+    def moved(block, shift):
+        return pltpu.roll(block, shift % 128, 1) if shift % 128 else block
+
+    left = [moved(packed[8 * (p // 4) : 8 * (p // 4) + 8], -32 * (p % 4)) for p in range(8)]
+    under = [jnp.where(lane < 32, left[4 + k], moved(packed[16:24], 32 - 32 * k)) for k in range(4)]
+    turned = jnp.transpose(jnp.concatenate((left[:4] + under) * 2, axis=0))
     parts = []
     for p in range(8):
-        side = packed if p < 4 else turned
-        at = 8 * (p % 4)
+        side = jnp.where(lane < 32, left[p], turned[8 * p : 8 * p + 8]) if p < 4 else under[p - 4]
         eye = (lane == inner + (K + 8 * p)).astype(F32)
-        parts.append(jnp.where(lane < K, side[at : at + 8], eye))
+        parts.append(jnp.where(lane < K, side, eye))
     out = []
     for p in range(8):
         block = parts[p]
@@ -109,7 +129,7 @@
 def kernel(
     row_any, col_any, count_any, tiles_any, start_any, lower_ref, both, piece_ref,
     places, count, inverse_v, inverse, tiles, x_ref, start, own, other, product, across, deep_in, pieces, pieces_in,
-    gram, gacross, gdeep, mid, partial, load_sem, send_sem, recv_sem,
+    gram, gacross, gdeep, gram_sum, mid, partial, load_sem, send_sem, recv_sem,
 ):
     y, x, z = (lax.axis_index(name) for name in CELL)
     core = lax.axis_index("gene")
@@ -206,8 +226,7 @@
             square = lax.dot_general(both[...], both[...], LANES, preferred_element_type=F32)
             square = square[:K] + square[K:]
             square = square + pltpu.roll(square, K, 1)
-            half = lax.broadcasted_iota(jnp.int32, (K // 2, 2 * K), 1) < K
-            packed = jnp.where(half, square[: K // 2], square[K // 2 :])
+            packed = pack(square)
             gram[r] = packed
             gacross[r, here] = packed
             for d in PLANE_ORDER:
@@ -224,25 +243,42 @@
             gdeep[r, z] = total
             for d in Z_ORDER:
                 gram_deep(r, d, 1).start()
-                gram_deep(r, d, 0).start()
-            gram_deep(r, 0, 0).start()
+                if r == 1:
+                    gram_deep(r, d, 0).start()
+            if r == 1:
+                gram_deep(r, 0, 0).start()
+
+    def gram_pair():
+        return copy_of(gram_sum, gram_sum, GDEEP + NZ, partner)
 
     def gram_end(r):
         @pl.when(core == 1)
         def _():
             for d in Z_ORDER:
                 gram_deep(r, d, 1).wait_recv()
+            if r == 0:
+                total = gdeep[r, 0]
+                for zz in range(1, NZ):
+                    total = total + gdeep[r, zz]
+                gram_sum[...] = total
+                gram_pair().start()
 
         @pl.when(core == 0)
         def _():
-            for d in range(NZ):
-                gram_deep(r, d, 0).wait_recv()
+            if r == 0:
+                gram_pair().wait_recv()
+            else:
+                for d in range(NZ):
+                    gram_deep(r, d, 0).wait_recv()
 
         @pl.when(z >= 0)
         def _():
-            total = gdeep[r, 0]
-            for zz in range(1, NZ):
-                total = total + gdeep[r, zz]
+            if r == 0:
+                total = gram_sum[...]
+            else:
+                total = gdeep[r, 0]
+                for zz in range(1, NZ):
+                    total = total + gdeep[r, zz]
             high, low = split(invert(total))
             lower_ref[...] = jnp.concatenate([high, high, low, low], axis=1)
 
@@ -277,9 +313,8 @@
                 send(0, d // NX, d % NX)
 
         for h in range(1, HALVES[r]):
-            for dy in (2, 1, 3, 0):
-                for dx in (2, 1, 3, 0):
-                    send(h, dy, dx)
+            for d in PLANE_ORDER:
+                send(h, d // NX, d % NX)
 
     def product_middle(r, h):
         for d in PLANE_ORDER:
@@ -303,8 +338,11 @@
                 gram_across(r, d).wait_send()
             for d in Z_ORDER:
                 gram_deep(r, d, 1).wait_send()
-            for d in range(NZ):
-                gram_deep(r, d, 0).wait_send()
+            if r == 0:
+                gram_pair().wait_send()
+            else:
+                for d in range(NZ):
+                    gram_deep(r, d, 0).wait_send()
 
     build(0)
     for i in range(CHUNKS):
@@ -424,9 +462,10 @@
             pltpu.VMEM((NZ, K, TILE), F32),
             pltpu.VMEM((NZ, 8, TILE), F32),
             pltpu.VMEM((NZ, 8, TILE), F32),
-            pltpu.VMEM((2, K // 2, 2 * K), F32),
-            pltpu.VMEM((2, PLANE, K // 2, 2 * K), F32),
-            pltpu.VMEM((2, NZ, K // 2, 2 * K), F32),
+            pltpu.VMEM((2, 24, 2 * K), F32),
+            pltpu.VMEM((2, PLANE, 24, 2 * K), F32),
+            pltpu.VMEM((2, NZ, 24, 2 * K), F32),
+            pltpu.VMEM((24, 2 * K), F32),
             pltpu.VMEM((PLANE, K, TILE), BF16),
             pltpu.VMEM((CHUNKS, K, CHUNK), F32),
             pltpu.SemaphoreType.DMA((5 + LOADS,)),

time: 58.1 us -> 57.2 us (0.985)
  Pallas kernels: 56.7 us -> 55.8 us
    pallas_call x1, Pallas kernels: 55.8 us -> 54.9 us  [local(): pl.pallas_call(kernel, out_shape=(pltpu.VMEM((K, 4 * K), BF16), pltpu.VME...]
where the time goes in v6:
time: 57.2 us; the launch traced here: 57.1 us
  Pallas kernels  55.8 us (98%)
  between operations  1.29 us (2%)
    pallas_call x1, Pallas kernels, local(): pl.pallas_call(kernel, out_shape=(pltpu.VMEM((K, 4 * K), BF16), pltpu.VME...  54.9 us

profile of v6, /device:TPU:1, one launch (start us, length us, event | category | flops | bytes accessed | tf_op | source)
XLA Modules:
  0.0 57.1 jit_solution(11218706327173737806)
XLA Ops:
  1.3 54.9 %shard_map.68 = (bf16[64,256]{1,0:T(8,128)(2,1)S(1)}, bf16[128,1024]{1,0:T(8,128)(2,1)S(1)}, f32[8,128]{1,0:T(8,128)S(1)}) custom-call(s32[1,64]{1,0:T(1,128)} %row_any.1, s32[1,64]{1,0:T(1,128)} %col_any.1, s32[1,1]{1,0:T(1,128)S(6)} %copy.7.count_any, bf16[64,128,128]{2,1,0:T(8,128)(2,1)} %bitcast.2, bf16[64,2048]{1,0:T(8,128)(2,1)} %start_any.1), custom_call_target="tpu_custom_call" | custom-call | tf_op jit(solution)/shard_map/pallas_call | solution.py:441
  56.2 0.9 %shard_map.69 = (bf16[64,1024]{1,0:T(8,128)(2,1)}, f32[16,64]{1,0:T(8,128)}) custom-call(bf16[64,256]{1,0:T(8,128)(2,1)S(1)} %get-tuple-element.7.lower_ref, bf16[128,1024]{1,0:T(8,128)(2,1)S(1)} %get-tuple-element.8.both_ref, f32[8,128]{1,0:T(8,128)S(1)} %get-tuple-element.9.piece_ref), custom_call_target="tpu_custom_call" | custom-call | tf_op jit(solution)/shard_map/pallas_call | solution.py:477

commit v7 on v6

--- a/solution.py
+++ b/solution.py
@@ -128,7 +128,7 @@
 
 def kernel(
     row_any, col_any, count_any, tiles_any, start_any, lower_ref, both, piece_ref,
-    places, count, inverse_v, inverse, tiles, x_ref, start, own, other, product, across, deep_in, pieces, pieces_in,
+    places, count, inverse_v, inverse, tiles, x_ref, xt_ref, start, own, other, product, across, deep_in, pieces, pieces_in,
     gram, gacross, gdeep, gram_sum, mid, partial, load_sem, send_sem, recv_sem,
 ):
     y, x, z = (lax.axis_index(name) for name in CELL)
@@ -157,7 +157,7 @@
 
     barrier = pltpu.get_barrier_semaphore()
     peers = [partner] + [in_plane(d) for d in range(1, PLANE)]
-    peers += [on_z(d, core) for d in range(1, NZ)] + [on_z(d, other_core) for d in range(1, NZ)]
+    peers += [on_z(d, which) for which in (core, other_core) for d in Z_ORDER]
     for peer in peers:
         pl.semaphore_signal(barrier, inc=1, device_id=peer, device_id_type=MESH)
 
@@ -197,15 +197,17 @@
     def chunk(r, i, scores_of):
         @pl.when(z >= 0)
         def _():
-            if r == 0 and i == 1:
-                pl.semaphore_wait(barrier, len(peers))
-            if i > 0:
+            if r == 1 and i > 0:
                 pair_copy(r, i - 1).start()
             if r == 0 and i + 1 < CHUNKS:
                 build(i + 1)
             own[r, i] = scores_of(i)
 
     def join(r):
+        if r == 0:
+            pl.semaphore_wait(barrier, len(peers))
+            for i in range(CHUNKS - 1):
+                pair_copy(r, i).start()
         pair_copy(r, CHUNKS - 1).start()
         for i in range(CHUNKS):
             pair_copy(r, i).wait_recv()
@@ -344,6 +346,18 @@
                 for d in range(NZ):
                     gram_deep(r, d, 0).wait_send()
 
+    def turn_over():
+        def column(c, carry):
+            for i in range(CHUNKS):
+                strip = jnp.concatenate(
+                    [jnp.transpose(x_ref[c, i * CHUNK + k * TILE : i * CHUNK + (k + 1) * TILE]) for k in range(CHUNK // TILE)],
+                    axis=1,
+                )
+                xt_ref[i, c] = strip
+            return carry
+
+        lax.fori_loop(0, COL_BLOCKS, column, 0)
+
     build(0)
     for i in range(CHUNKS):
         chunk(
@@ -354,6 +368,7 @@
     join(0)
     gram_start(0)
     product_start(0)
+    turn_over()
     gram_middle(0)
     def whole_copy(h, d):
         rows = pl.ds(h * K // HALVES[0], K // HALVES[0])
@@ -385,7 +400,8 @@
         at = [NX * lax.rem(y + NY - d // NX, NY) + lax.rem(x + NX - d % NX, NX) for d in offsets]
         return lax.dot_general(
             jnp.concatenate([mid[n] for n in at], axis=1),
-            cells_of(i, at), LANES, preferred_element_type=F32,
+            jnp.concatenate([xt_ref[i, n] for n in at], axis=0), (((1,), (0,)), ((), ())),
+            preferred_element_type=F32,
         )
 
     near, far = [0] + PLANE_ORDER[:3:-1], PLANE_ORDER[:4]
@@ -454,6 +470,7 @@
             pltpu.SMEM((1, ROW_BLOCKS * COL_BLOCKS), jnp.int32),
             pltpu.VMEM((SLOTS + 1, TILE, TILE), BF16),
             pltpu.VMEM((COL_BLOCKS, CELLS, TILE), BF16),
+            pltpu.VMEM((CHUNKS, COL_BLOCKS, TILE, CHUNK), BF16),
             pltpu.VMEM((K, GENES), BF16),
             pltpu.VMEM((2, CHUNKS, K, CHUNK), F32),
             pltpu.VMEM((2, CHUNKS, K, CHUNK), F32),

time: 57.2 us -> 56.1 us (0.981)
  Pallas kernels: 55.8 us -> 54.7 us
    pallas_call x1, Pallas kernels: 54.9 us -> 53.8 us  [local(): pl.pallas_call(kernel, out_shape=(pltpu.VMEM((K, 4 * K), BF16), pltpu.VME...]
where the time goes in v7:
time: 56.1 us; the launch traced here: 55.9 us
  Pallas kernels  54.7 us (98%)
  between operations  1.29 us (2%)
    pallas_call x1, Pallas kernels, local(): pl.pallas_call(kernel, out_shape=(pltpu.VMEM((K, 4 * K), BF16), pltpu.VME...  53.8 us

profile of v7, /device:TPU:1, one launch (start us, length us, event | category | flops | bytes accessed | tf_op | source)
XLA Modules:
  0.0 55.9 jit_solution(9326504684277596717)
XLA Ops:
  1.3 53.8 %shard_map.68 = (bf16[64,256]{1,0:T(8,128)(2,1)S(1)}, bf16[128,1024]{1,0:T(8,128)(2,1)S(1)}, f32[8,128]{1,0:T(8,128)S(1)}) custom-call(s32[1,64]{1,0:T(1,128)} %row_any.1, s32[1,64]{1,0:T(1,128)} %col_any.1, s32[1,1]{1,0:T(1,128)S(6)} %copy.7.count_any, bf16[64,128,128]{2,1,0:T(8,128)(2,1)} %bitcast.2, bf16[64,2048]{1,0:T(8,128)(2,1)} %start_any.1), custom_call_target="tpu_custom_call" | custom-call | tf_op jit(solution)/shard_map/pallas_call | solution.py:457
  55.1 0.9 %shard_map.69 = (bf16[64,1024]{1,0:T(8,128)(2,1)}, f32[16,64]{1,0:T(8,128)}) custom-call(bf16[64,256]{1,0:T(8,128)(2,1)S(1)} %get-tuple-element.7.lower_ref, bf16[128,1024]{1,0:T(8,128)(2,1)S(1)} %get-tuple-element.8.both_ref, f32[8,128]{1,0:T(8,128)S(1)} %get-tuple-element.9.piece_ref), custom_call_target="tpu_custom_call" | custom-call | tf_op jit(solution)/shard_map/pallas_call | solution.py:494

commit v8 on v7

--- a/solution.py
+++ b/solution.py
@@ -225,8 +225,9 @@
     def gram_start(r):
         @pl.when(core == 1)
         def _():
-            square = lax.dot_general(both[...], both[...], LANES, preferred_element_type=F32)
-            square = square[:K] + square[K:]
+            halves = [both[:, i * CHUNK : (i + 1) * CHUNK] for i in range(CHUNKS)]
+            squares = [lax.dot_general(half, half, LANES, preferred_element_type=F32) for half in halves]
+            square = sum(part[:K] + part[K:] for part in squares)
             square = square + pltpu.roll(square, K, 1)
             packed = pack(square)
             gram[r] = packed
@@ -407,9 +408,9 @@
     near, far = [0] + PLANE_ORDER[:3:-1], PLANE_ORDER[:4]
     for d in near[1:]:
         spread_copy(d).wait_recv()
-    for i in range(CHUNKS):
-        @pl.when(z >= 0)
-        def _():
+    @pl.when(z >= 0)
+    def _():
+        for i in range(CHUNKS):
             partial[i] = scores_with(i, near)
 
     for d in far:

time: 56.1 us -> 56.1 us (level)
  no operation moved by 1% of the time
where the time goes in v8:
time: 56.1 us; the launch traced here: 55.9 us
  Pallas kernels  54.7 us (98%)
  between operations  1.29 us (2%)
    pallas_call x1, Pallas kernels, local(): pl.pallas_call(kernel, out_shape=(pltpu.VMEM((K, 4 * K), BF16), pltpu.VME...  53.8 us

profile of v8, /device:TPU:1, one launch (start us, length us, event | category | flops | bytes accessed | tf_op | source)
XLA Modules:
  0.0 55.9 jit_solution(9326504684277596717)
XLA Ops:
  1.3 53.8 %shard_map.68 = (bf16[64,256]{1,0:T(8,128)(2,1)S(1)}, bf16[128,1024]{1,0:T(8,128)(2,1)S(1)}, f32[8,128]{1,0:T(8,128)S(1)}) custom-call(s32[1,64]{1,0:T(1,128)} %row_any.1, s32[1,64]{1,0:T(1,128)} %col_any.1, s32[1,1]{1,0:T(1,128)S(6)} %copy.7.count_any, bf16[64,128,128]{2,1,0:T(8,128)(2,1)} %bitcast.2, bf16[64,2048]{1,0:T(8,128)(2,1)} %start_any.1), custom_call_target="tpu_custom_call" | custom-call | tf_op jit(solution)/shard_map/pallas_call | solution.py:458
  55.1 0.9 %shard_map.69 = (bf16[64,1024]{1,0:T(8,128)(2,1)}, f32[16,64]{1,0:T(8,128)}) custom-call(bf16[64,256]{1,0:T(8,128)(2,1)S(1)} %get-tuple-element.7.lower_ref, bf16[128,1024]{1,0:T(8,128)(2,1)S(1)} %get-tuple-element.8.both_ref, f32[8,128]{1,0:T(8,128)S(1)} %get-tuple-element.9.piece_ref), custom_call_target="tpu_custom_call" | custom-call | tf_op jit(solution)/shard_map/pallas_call | solution.py:495
